TPU v7x, 32 devices: a whole 2x2x4 slice. The times are simulated.
32 devices in a mesh: row: 8 (over z, core), col: 4 (over y, x).
Axes of the slice: x: 2, y: 2, z: 4, core: 2. Of those that a mesh axis runs over, the one named last changes fastest.
Arguments:
- matrix: float32 [12288, 12288], P('row', 'col'), may hold values from -8 to 8
Outputs:
- updated: float32 [12288, 12288], P('row', 'col')
- reflectors: float32 [16, 12288], replicated
- coefficients: float32 [2, 16], replicated
All inputs are finite; a program needn't handle non-finite values.
Results may differ from a plain program's by a relative error of at most 0.0003.
Values sent between devices are 32-bit elements; how exact they have to be, the bound alone decides.
A program may use at most 64 MiB of HBM per device.

v0:
```python
import jax
import jax.numpy as jnp
from jax import lax
from jax.experimental import pallas as pl
from jax.experimental.pallas import tpu as pltpu
from jax.sharding import PartitionSpec as P

K = 16
HEAD = 24
LANES = 128
MESH = pl.DeviceIdType.MESH


def lane_pick(block, lanes, index):
    return jnp.sum(jnp.where(lanes == index, block, 0.0), axis=1, keepdims=True)


def panel_kernel(rows, cols, n_row, n_col, mat, v_out, wc_out, vw_out, coef_out, kap_out,
                 tile, first, panel, vw, msg, recv, gout, c0_ref, u_ref, p_ref, au_ref, b0_ref,
                 vu_ref, wu_ref, s_ref, kmsg, krecv,
                 load_sem, first_sem, panel_sem, head_sem, psend_sem, send_sem, recv_sem, gsend_sem, v_sem, w_sem,
                 ksend_sem, k_sem):
    width = rows + LANES
    halves = cols // rows
    r = lax.axis_index("row")
    c = lax.axis_index("col")
    blocks = rows // LANES
    ctiles = cols // LANES

    def chunk(i):
        part = pl.ds(pl.multiple_of(i * LANES, LANES), LANES)
        return pltpu.make_async_copy(mat.at[part], tile.at[part], load_sem.at[i])

    def start_chunk(i, carry):
        chunk(i).start()
        return carry

    first_copy = pltpu.make_async_copy(mat.at[:, 0:LANES], first, first_sem)
    pl.when(c == 0)(lambda: first_copy.start())
    lax.fori_loop(0, blocks, start_chunk, 0)

    barrier = pltpu.get_barrier_semaphore()
    for dr in range(n_row):
        for dc in range(n_col):
            if dr or dc:
                pl.semaphore_signal(barrier, inc=1, device_id=(lax.rem(r + dr, n_row), lax.rem(c + dc, n_col)),
                                    device_id_type=MESH)

    @pl.when(c == 0)
    def _():
        first_copy.wait()
        for i in range(blocks):
            part = slice(i * LANES, (i + 1) * LANES)
            panel[:, part] = first[part, :].T[0:HEAD, :]

    vw[...] = jnp.zeros_like(vw)
    u_ref[...] = jnp.zeros_like(u_ref)
    p_ref[...] = jnp.zeros_like(p_ref)
    au_ref[...] = jnp.zeros_like(au_ref)
    vu_ref[...] = jnp.zeros_like(vu_ref)
    wu_ref[...] = jnp.zeros_like(wu_ref)
    s_ref[...] = jnp.zeros_like(s_ref)
    coef_out[...] = jnp.zeros_like(coef_out)
    pl.semaphore_wait(barrier, n_row * n_col - 1)

    def panel_copy(dc):
        return pltpu.make_async_remote_copy(
            panel.at[:, 0:rows], panel.at[:, 0:rows], psend_sem, panel_sem,
            device_id=(r, dc), device_id_type=MESH)

    def head_copy(dr, dc):
        src = mat.at[0:HEAD, 0:LANES]
        dst = panel.at[:, rows:width]
        if dr == 0 and dc == 0:
            return pltpu.make_async_copy(src, dst, head_sem)
        return pltpu.make_async_remote_copy(src, dst, psend_sem, head_sem, device_id=(dr, dc), device_id_type=MESH)

    def each_target(fn_remote, fn_local):
        for dc in range(n_col):
            for h in range(halves):
                if dc:
                    fn_remote(h, dc)
                else:
                    own = halves * c + h == r
                    pl.when(jnp.logical_not(own))(lambda h=h, dc=dc: fn_remote(h, dc))
                    if fn_local is not None:
                        pl.when(own)(lambda h=h, dc=dc: fn_local(h, dc))

    @pl.when(c == 0)
    def _():
        @pl.when(r == 0)
        def _():
            for dr in reversed(range(n_row)):
                for dc in reversed(range(n_col)):
                    head_copy(dr, dc).start()
        for dc in reversed(range(1, n_col)):
            panel_copy(dc).start()

    pltpu.make_async_copy(panel.at[:, rows:width], panel.at[:, rows:width], head_sem).wait()

    @pl.when(c != 0)
    def _():
        pltpu.make_async_copy(panel.at[:, 0:rows], panel.at[:, 0:rows], panel_sem).wait()

    c0_ref[...] = panel[0:1, :]
    lane = lax.broadcasted_iota(jnp.int32, (1, width), 1)
    pos = jnp.where(lane < rows, lane + r * rows, jnp.where(lane < rows + HEAD, lane - rows, -1))
    l128 = lax.broadcasted_iota(jnp.int32, (1, LANES), 1)
    k16 = lax.broadcasted_iota(jnp.int32, (K, 1), 0)

    def send_copy(j, h, dc, local):
        src = msg.at[j, h]
        dst = recv.at[j, r]
        if local:
            return pltpu.make_async_copy(src, dst, recv_sem.at[j])
        return pltpu.make_async_remote_copy(
            src, dst, send_sem, recv_sem.at[j],
            device_id=(halves * c + h, lax.rem(c + dc, n_col)), device_id_type=MESH)

    def v_copy(j, dr):
        return pltpu.make_async_remote_copy(
            gout.at[j, 0], v_out.at[j, r], gsend_sem, v_sem,
            device_id=(lax.rem(r + dr, n_row), c), device_id_type=MESH)

    def w_copy(j, dr):
        return pltpu.make_async_remote_copy(
            gout.at[j, 1], wc_out.at[j, lax.rem(r, halves)], gsend_sem, w_sem,
            device_id=(lax.rem(r + dr, n_row), c), device_id_type=MESH)

    def k_copy(dr):
        return pltpu.make_async_remote_copy(
            kmsg, krecv.at[r], ksend_sem, k_sem,
            device_id=(lax.rem(r + dr, n_row), c), device_id_type=MESH)

    gives_w = r // halves == c

    def spread(i):
        row = b0_ref[:, pl.ds(pl.multiple_of(i * LANES, LANES), LANES)]
        return jnp.broadcast_to(row, (LANES, LANES)).T

    def step(j, carry):
        m2 = pos > j + 1
        c0 = c0_ref[...]
        b0 = jnp.where(m2, c0, 0.0)
        b0_ref[...] = b0
        u_prev = u_ref[...]
        p_prev = p_ref[...]

        b_loc = b0[:, :rows]
        dvw = jnp.sum(vw[:, :rows] * b_loc, axis=1, keepdims=True)
        dpn = jnp.sum(panel[:, :rows] * b_loc, axis=1, keepdims=True)
        n0 = jnp.sum(b_loc * b_loc, axis=1, keepdims=True)
        kp = jnp.sum(u_prev[:, :rows] * p_prev[:, :rows], axis=1, keepdims=True)
        s32 = lax.broadcasted_iota(jnp.int32, (2 * K, LANES), 0)
        t32 = lax.broadcasted_iota(jnp.int32, (2 * K, LANES), 1)
        s24 = lax.broadcasted_iota(jnp.int32, (HEAD, LANES), 0)
        t24 = lax.broadcasted_iota(jnp.int32, (HEAD, LANES), 1)
        sc = jnp.sum(jnp.where(s32 == t32, dvw, 0.0), axis=0, keepdims=True)
        sc += jnp.sum(jnp.where(s24 + 2 * K == t24, dpn, 0.0), axis=0, keepdims=True)
        sc += jnp.where(l128 == 2 * K + HEAD, n0, 0.0) + jnp.where(l128 == 2 * K + HEAD + 1, kp, 0.0)

        def block(i, state):
            bc, accs = state
            pl.when(j == 0)(lambda: chunk(i).wait())
            nxt = spread(jnp.minimum(i + 1, blocks - 1))
            b3 = bc.reshape(LANES // 8, 8, LANES)
            part = pl.ds(pl.multiple_of(i * LANES, LANES), LANES)
            new = []
            for t in range(ctiles):
                x = tile[part, t * LANES:(t + 1) * LANES].reshape(LANES // 8, 8, LANES)
                new.append(accs[t] + jnp.sum(x * b3, axis=0))
            return nxt, tuple(new)

        zero = jnp.zeros((8, LANES), jnp.float32)
        _, accs = lax.fori_loop(0, blocks, block, (spread(0), (zero,) * ctiles))
        per = rows // LANES
        for h in range(halves):
            for t in range(per):
                msg[j, h, :, t * LANES:(t + 1) * LANES] = jnp.sum(accs[h * per + t], axis=0, keepdims=True)
            msg[j, h, :, rows:width] = sc

        each_target(lambda h, dc: send_copy(j, h, dc, False).start(), lambda h, dc: send_copy(j, h, dc, True).start())
        pltpu.make_async_copy(recv.at[j], recv.at[j], recv_sem.at[j]).wait()

        tot = jnp.sum(recv[j], axis=0)
        sc = tot[:, rows:width]
        wide = jnp.broadcast_to(sc, (2 * K, LANES))
        dots = jnp.sum(jnp.where(s32 == t32, wide, 0.0), axis=1, keepdims=True)
        n0 = sc[:, 2 * K + HEAD:2 * K + HEAD + 1]
        kp = sc[:, 2 * K + HEAD + 1:2 * K + HEAD + 2]
        tau_prev = s_ref[0:1, 0:1]
        bb_prev = s_ref[1:2, 0:1]
        kap = 0.5 * tau_prev * kp
        kap_out[pl.ds(j, 1), :] = jnp.broadcast_to(kap, (1, LANES))
        vw[pl.ds(K + j - 1, 1), :] = p_prev - kap * u_prev
        pj = panel[pl.ds(j, 1), :]
        pj1 = panel[pl.ds(j + 1, 1), :]
        col = c0 + 2.0 * kap * u_prev
        uj1 = lane_pick(u_prev[:, rows:width], l128, j + 1)
        aq = au_ref[...] - pj - uj1 * pj1
        yhead = jnp.where(l128 < HEAD, pltpu.roll(sc, LANES - 2 * K, 1), 0.0)
        y = jnp.concatenate([tot[:, :rows], yhead], axis=1) + 2.0 * kap * aq
        vb = dots[:K]
        wb = dots[K:]
        last = k16 == j - 1
        n1 = jnp.sum(jnp.where(last, vb, 0.0), axis=0, keepdims=True)
        b2 = jnp.maximum(n0 + 4.0 * kap * (n1 + kap * (bb_prev - uj1 * uj1)), 0.0)
        lead = lane_pick(col[:, rows:width], l128, j + 1)
        sig = jnp.sqrt(b2 + lead * lead)
        inv = 1.0 / (lead + sig)
        tau = 1.0 + lead / sig
        u = jnp.where(m2, col * inv, 0.0) + jnp.where(pos == j + 1, 1.0, 0.0)
        au = y * inv + pj1

        head = vw[:, rows:width]
        hj = lane_pick(head, l128, j)
        hj1 = lane_pick(head, l128, j + 1)
        uu = bb_prev + 1.0
        vup = jnp.where(last, uu, vu_ref[:, 0:1])
        wup = jnp.where(last, kp - kap * uu, wu_ref[:, 0:1])
        wb = jnp.where(last, wb - kap * vb, wb)
        vu = (vb + 2.0 * kap * (vup - hj[:K] - uj1 * hj1[:K])) * inv + hj1[:K]
        wu = (wb + 2.0 * kap * (wup - hj[K:] - uj1 * hj1[K:])) * inv + hj1[K:]
        v_all = vw[0:K, :]
        w_all = vw[K:2 * K, :]
        p = tau * (au - jnp.sum(v_all * wu + w_all * vu, axis=0, keepdims=True))
        pj1_entry = lane_pick(p[:, rows:width], l128, j + 1)
        c0n = pj1 - jnp.sum(v_all * hj1[K:] + w_all * hj1[:K], axis=0, keepdims=True) - pj1_entry * u - p
        gout[j, 0] = u[:, :rows]
        gout[j, 1] = p[:, :rows]
        c0_ref[...] = c0n
        u_ref[...] = u
        p_ref[...] = p
        au_ref[...] = au
        vu_ref[...] = jnp.broadcast_to(vu, (K, LANES))
        wu_ref[...] = jnp.broadcast_to(wu, (K, LANES))
        s_ref[0:1, :] = jnp.broadcast_to(tau, (1, LANES))
        s_ref[1:2, :] = jnp.broadcast_to(b2 * inv * inv, (1, LANES))
        coef_out[0:1, :] = jnp.where(l128 == j, tau, coef_out[0:1, :])
        coef_out[1:2, :] = jnp.where(l128 == j, -sig, coef_out[1:2, :])
        vw[pl.ds(j, 1), :] = u
        vw[pl.ds(K + j, 1), :] = p

        for dr in range(1, n_row):
            v_copy(j, dr).start()
        pltpu.make_async_copy(gout.at[j, 0], v_out.at[j, r], v_sem).start()

        @pl.when(gives_w)
        def _():
            for dr in range(1, n_row):
                w_copy(j, dr).start()
            pltpu.make_async_copy(gout.at[j, 1], wc_out.at[j, lax.rem(r, halves)], w_sem).start()
        return carry

    lax.fori_loop(0, K, step, 0)

    u = u_ref[...]
    p = p_ref[...]
    kp = jnp.sum(u[:, :rows] * p[:, :rows], axis=1, keepdims=True)
    kmsg[...] = jnp.broadcast_to(kp, (1, LANES))
    for dr in range(1, n_row):
        k_copy(dr).start()
    pltpu.make_async_copy(kmsg, krecv.at[r], k_sem).start()
    pltpu.make_async_copy(krecv, krecv, k_sem).wait()
    kap = 0.5 * s_ref[0:1, :] * jnp.sum(krecv[...], axis=0)
    kap_out[K:K + 1, :] = kap
    vw[2 * K - 1:2 * K, :] = p - kap[:, 0:1] * u
    vw_out[...] = vw[:, :rows]

    def drain(j, carry):
        each_target(lambda h, dc: send_copy(j, h, dc, False).wait_send(), None)
        for dr in range(1, n_row):
            v_copy(j, dr).wait_send()

        @pl.when(gives_w)
        def _():
            for dr in range(1, n_row):
                w_copy(j, dr).wait_send()
        return carry

    lax.fori_loop(0, K, drain, 0)

    @pl.when(c == 0)
    def _():
        @pl.when(r == 0)
        def _():
            for dr in range(n_row):
                for dc in range(n_col):
                    if dr or dc:
                        head_copy(dr, dc).wait_send()
        for dc in range(1, n_col):
            panel_copy(dc).wait_send()

    for dr in range(1, n_row):
        k_copy(dr).wait_send()
    pltpu.make_async_copy(v_out, v_out, v_sem).wait()
    pltpu.make_async_copy(wc_out, wc_out, w_sem).wait()


def pieces(x):
    hi = lax.reduce_precision(x, 8, 7)
    rest = x - hi
    mid = lax.reduce_precision(rest, 8, 7)
    low = lax.reduce_precision(rest - mid, 8, 7)
    return [part.astype(jnp.bfloat16) for part in (hi, mid, low)]


def make_per_device(n_row, n_col):
    def per_device(matrix):
        rows, cols = matrix.shape
        halves = cols // rows
        width = rows + LANES
        f32 = jnp.float32
        vmem = pl.BlockSpec(memory_space=pltpu.VMEM)
        anyspace = pl.BlockSpec(memory_space=pl.ANY)
        dma = pltpu.SemaphoreType.DMA

        def kernel(*refs):
            panel_kernel(rows, cols, n_row, n_col, *refs)

        v_full, wc, vw, coef, kap = pl.pallas_call(
            kernel,
            out_shape=(
                jax.ShapeDtypeStruct((K, n_row, 1, rows), f32),
                jax.ShapeDtypeStruct((K, halves, 1, rows), f32),
                jax.ShapeDtypeStruct((2 * K, rows), f32),
                jax.ShapeDtypeStruct((2, LANES), f32),
                jax.ShapeDtypeStruct((K + 1, LANES), f32),
            ),
            in_specs=[anyspace],
            out_specs=(anyspace, anyspace, vmem, vmem, vmem),
            scratch_shapes=[
                pltpu.VMEM((rows, cols), f32),
                pltpu.VMEM((rows, LANES), f32),
                pltpu.VMEM((HEAD, width), f32),
                pltpu.VMEM((2 * K, width), f32),
                pltpu.VMEM((K, halves, 1, width), f32),
                pltpu.VMEM((K, n_row, 1, width), f32),
                pltpu.VMEM((K, 2, 1, rows), f32),
                pltpu.VMEM((1, width), f32),
                pltpu.VMEM((1, width), f32),
                pltpu.VMEM((1, width), f32),
                pltpu.VMEM((1, width), f32),
                pltpu.VMEM((1, width), f32),
                pltpu.VMEM((K, LANES), f32),
                pltpu.VMEM((K, LANES), f32),
                pltpu.VMEM((8, LANES), f32),
                pltpu.VMEM((1, LANES), f32),
                pltpu.VMEM((n_row, 1, LANES), f32),
                dma((rows // LANES,)),
                dma, dma, dma, dma, dma,
                dma((K,)),
                dma, dma, dma, dma, dma,
            ],
            compiler_params=pltpu.CompilerParams(
                collective_id=0, has_side_effects=True, vmem_limit_bytes=48 * 1024 * 1024),
        )(matrix)
        reflectors = v_full.reshape(K, n_row * rows)
        c = lax.axis_index("col")
        v_cols = lax.dynamic_slice_in_dim(reflectors, c * cols, cols, 1)
        w_cols = wc.reshape(K, cols) - kap[1:, 0:1] * v_cols
        left = pieces(vw)
        right = pieces(jnp.concatenate([w_cols, v_cols], axis=0))
        order = ((0, 0), (0, 1), (1, 0), (1, 1), (0, 2), (2, 0))
        big_left = jnp.concatenate([left[a] for a, _ in order], axis=0)
        big_right = jnp.concatenate([right[b] for _, b in order], axis=0)
        change = lax.dot_general(big_left, big_right, (((0,), (0,)), ((), ())), preferred_element_type=f32)
        return matrix - change, reflectors, coef[:, :K]
    return per_device


def solution(mesh):
    return jax.shard_map(
        make_per_device(mesh.shape["row"], mesh.shape["col"]),
        mesh=mesh,
        in_specs=(P("row", "col"),),
        out_specs=(P("row", "col"), P(), P()),
        check_vma=False,
    )
```

profile of v0, /device:TPU:0, one launch (start us, length us, event | category | flops | bytes accessed | tf_op | source)
XLA Modules:
  0.0 160.9 jit_solution(1245821992768311875)
XLA Ops:
  0.6 143.4 %shard_map.38 = (f32[16,8,1,1536]{3,2,1,0:T(1,128)S(1)}, f32[16,2,1,1536]{3,2,1,0:T(1,128)S(1)}, f32[32,1536]{1,0:T(8,128)S(1)}, f32[2,128]{1,0:T(2,128)S(1)}, f32[17,128]{1,0:T(8,128)S(1)}) custom-call(f32[1536,3072]{1,0:T(8,128)} %refs_0_.1), custom_call_target="tpu_custom_call" | custom-call | tf_op jit(solution)/shard_map/pallas_call | solution.py:321
  144.0 0.6 reduce
  144.6 1.9 %reduce.2 = f32[16,8,1536]{2,1,0:T(8,128)S(1)} reduce(f32[16,8,1,1536]{3,2,1,0:T(1,128)S(1)} %get-tuple-element.11, f32[]{:T(128)} %constant.10), dimensions={2}, to_apply=%get-tuple-element.11.reduce_sub_computation | reduce | bytes 1572868 | tf_op jit(solution)/shard_map/pallas_call | solution.py:321
  146.5 0.5 copy.5
  147.0 0.0 copy-start
  147.0 0.1 slice_reduce_fusion
  147.1 0.1 multiply_subtract_fusion
  147.3 0.5 copy-done
  148.1 0.1 fusion.4
  148.2 12.1 %convolution_subtract_fusion = f32[1536,3072]{1,0:T(8,128)} fusion(f32[1536,3072]{1,0:T(8,128)} %refs_0_.1, bf16[192,1536]{1,0:T(8,128)(2,1)S(1)} %fusion.5, bf16[192,3072]{1,0:T(8,128)(2,1)S(1)} %constant_dynamic-update-slice_fusion.5), kind=kOutput, calls=%fused_computation | convolution fusion | flops 1816657920 | bytes 39518208 | tf_op jit(solution)/shard_map/dot_general | solution.py:367
  160.3 0.6 copy.17
  (12 shorter events, 0.3 us)
Async XLA Ops:
  147.0 0.9 copy-start
where the time goes:
time: 161 us
  Pallas kernels  143 us (89%)
  matrix products  12.1 us (8%)
  other arithmetic  2.86 us (2%)
  local copies, waits for them, and re-layouts  1.69 us (1%)
    pallas_call x1, Pallas kernels, per_device(): pl.pallas_call(kernel, out_shape=(jax.ShapeDtypeStruct((K, n_row, 1, rows...  143 us
    dot_general x1, matrix products, per_device(): lax.dot_general(big_left, big_right, (((0,), (0,)), ((), ())), preferred_...  12.1 us

commit v1 on v0

v1 whole, which is shorter than its diff:
```python
import jax
import jax.numpy as jnp
from jax import lax
from jax.experimental import pallas as pl
from jax.experimental.pallas import tpu as pltpu
from jax.sharding import PartitionSpec as P

K = 16
PAIRS = K // 2
HEAD = 24
LANES = 128
SUB = 8
GROUPS = LANES // SUB
MESH = pl.DeviceIdType.MESH
F32 = jnp.float32


def lanes_of(t):
    return slice(t * LANES, (t + 1) * LANES)


def spread_row(row):
    return jnp.broadcast_to(row, (LANES, LANES)).T


def panel_kernel(rows, cols, n_row, n_col, mat, tile, refl, vwr, vwc, coef,
                 headrows, phead, rowc, vout,
                 sum_a, sum_b, sc_a, sc_b, red_a, red_b, hd_a, hd_b,
                 c0r, ur, pr, aur, c0c, uc, pc, auc, c0h, uh, ph, auh, vwh,
                 coefc, coefp, vuwu, scal, b0r, b0c, xs, accs, dacc,
                 load_sem, hrow_sem, head_sem, row_sem, v_sem,
                 ya_sem, sa_sem, ra_sem, ha_sem, yb_sem, sb_sem, rb_sem, hb_sem,
                 ssem):
    halves = cols // rows
    r = lax.axis_index("row")
    c = lax.axis_index("col")
    blocks = rows // LANES
    ctiles = cols // LANES
    rtiles = rows // LANES
    half_tiles = ctiles // 2
    half_blocks = blocks // 2
    diag = r // halves == c
    own_half = lax.rem(r, halves)

    def along_row(dr):
        return (lax.rem(r + dr, n_row), c)

    def along_col(dc):
        return (r, lax.rem(c + dc, n_col))

    def remote(src, dst, sem, device):
        return pltpu.make_async_remote_copy(src, dst, ssem, sem, device_id=device, device_id_type=MESH)

    def landed(ref, sem):
        pltpu.make_async_copy(ref, ref, sem).wait()

    def to_rows(ref, sem):
        for dr in range(1, n_row):
            remote(ref, ref, sem, along_row(dr)).start()

    def to_cols(ref, sem):
        for dc in range(1, n_col):
            remote(ref, ref, sem, along_col(dc)).start()

    def chunk(i):
        part = pl.ds(pl.multiple_of(i * LANES, LANES), LANES)
        return pltpu.make_async_copy(mat.at[part], tile.at[part], load_sem.at[i])

    hrow_copy = pltpu.make_async_copy(mat.at[0:HEAD], headrows, hrow_sem)
    pl.when(r == 0)(lambda: hrow_copy.start())

    def start_chunk(i, carry):
        chunk(i).start()
        return carry

    lax.fori_loop(0, blocks, start_chunk, 0)

    barrier = pltpu.get_barrier_semaphore()
    for dr in range(n_row):
        for dc in range(n_col):
            if dr or dc:
                pl.semaphore_signal(barrier, inc=1, device_id=(lax.rem(r + dr, n_row), lax.rem(c + dc, n_col)),
                                    device_id_type=MESH)

    for ref in (vwr, vwc, vwh, c0r, ur, pr, aur, uc, pc, auc, c0h, uh, ph, auh, coefc, coefp, vuwu, scal, dacc, coef):
        ref[...] = jnp.zeros_like(ref)

    @pl.when(r == 0)
    def _():
        hrow_copy.wait()
        rowc[0] = headrows[0:1, :]
        rowc[1] = headrows[1:2, :]

    pl.semaphore_wait(barrier, n_row * n_col - 1)

    @pl.when(r == 0)
    def _():
        to_rows(rowc.at[0:2], row_sem.at[0])

        @pl.when(c == 0)
        def _():
            phead[...] = headrows[:, 0:LANES]
            for dr in range(n_row):
                for dc in range(n_col):
                    if dr or dc:
                        remote(headrows.at[:, 0:LANES], phead, head_sem,
                               (lax.rem(r + dr, n_row), lax.rem(c + dc, n_col))).start()

    @pl.when(r != 0)
    def _():
        landed(rowc.at[0:2], row_sem.at[0])

    c0c[...] = rowc[0]

    lane_r = lax.broadcasted_iota(jnp.int32, (1, rows), 1)
    lane_c = lax.broadcasted_iota(jnp.int32, (1, cols), 1)
    l128 = lax.broadcasted_iota(jnp.int32, (1, LANES), 1)
    pos_r = lane_r + r * rows
    pos_c = lane_c + c * cols
    k16 = lax.broadcasted_iota(jnp.int32, (K, LANES), 0)
    s40 = lax.broadcasted_iota(jnp.int32, (2 * K + SUB, LANES), 0)
    t40 = lax.broadcasted_iota(jnp.int32, (2 * K + SUB, LANES), 1)
    eye40 = s40 == t40
    diag3 = (lax.broadcasted_iota(jnp.int32, (GROUPS, SUB, LANES), 0) * SUB
             + lax.broadcasted_iota(jnp.int32, (GROUPS, SUB, LANES), 1)
             == lax.broadcasted_iota(jnp.int32, (GROUPS, SUB, LANES), 2))

    def srow(k):
        return scal[k:k + 1, :]

    def wide(x, n):
        return x if n == 1 else jnp.concatenate([x] * n, axis=1)

    def advance(j, vw, c0, u, p, au_ref, au_new, row_new, pos):
        tau, kap, e, inv = srow(0), srow(1), srow(2), srow(3)
        cc = coefc[...]
        cp = coefp[...]
        hot = jnp.where(j >= 0, j + 1, -1)
        last = jnp.maximum(j, 0)
        wrow, vrow, prow = [], [], []
        for t in range(c0.shape[1] // LANES):
            sl = lanes_of(t)
            x = vw[:, sl]
            au = au_new(t)
            row = row_new(t)
            ta = tau * au
            c0n = row - ta + jnp.sum(x * cc, axis=0, keepdims=True)
            pn = ta - jnp.sum(x * cp, axis=0, keepdims=True)
            u_old = u[:, sl]
            un = jnp.where(pos[:, sl] > j + 1, (c0[:, sl] + e * u_old) * inv, 0.0)
            un = jnp.where(pos[:, sl] == hot, 1.0, un)
            wrow.append(p[:, sl] - kap * u_old)
            vrow.append(un)
            prow.append(pn)
            c0[:, sl] = c0n
            u[:, sl] = un
            p[:, sl] = pn
            au_ref[:, sl] = au
        vw[pl.ds(K + j - 1, 1), :] = jnp.concatenate(wrow, axis=1)
        vw[pl.ds(last, 1), :] = jnp.concatenate(vrow, axis=1)
        vw[pl.ds(K + j, 1), :] = jnp.concatenate(prow, axis=1)

    def dots_add(vw, x_ref, u, p, t):
        sl = pl.ds(pl.multiple_of(t * LANES, LANES), LANES)
        x = x_ref[:, sl]
        dacc[0:2 * K, :] += vw[:, sl] * x
        dacc[2 * K:2 * K + 1, :] += x * x
        dacc[2 * K + 1:2 * K + 2, :] += u[:, sl] * p[:, sl]

    def dots_row():
        d = jnp.sum(dacc[...], axis=1, keepdims=True)
        out = jnp.sum(jnp.where(eye40, d, 0.0), axis=0, keepdims=True)
        dacc[...] = jnp.zeros_like(dacc)
        return out

    def matvec_cols(i, j):
        b0c[...] = jnp.where(pos_c > j + 1, c0c[...], 0.0)
        xb = [jnp.broadcast_to(b0c[:, lanes_of(t)], (SUB, LANES)) for t in range(ctiles)]
        per = ctiles // half_blocks

        def reduce_block(k):
            part = pl.ds(pl.multiple_of(k * LANES, LANES), LANES)
            a = accs[part, :].reshape(GROUPS, SUB, LANES)
            s = jnp.sum(a, axis=2, keepdims=True)
            row = jnp.sum(jnp.sum(jnp.where(diag3, s, 0.0), axis=0), axis=0, keepdims=True)
            sum_b[i, c, :, pl.ds(pl.multiple_of(k * LANES, LANES), LANES)] = row

        def block(first):
            def body(k, carry):
                pl.when(i == 0)(lambda: chunk(k).wait())
                part = pl.ds(pl.multiple_of(k * LANES, LANES), LANES)
                reduce_block(jnp.maximum(k - 1, 0))
                acc = jnp.zeros((GROUPS, SUB, LANES), F32)
                for t in range(ctiles):
                    acc = acc + tile[part, lanes_of(t)].reshape(GROUPS, SUB, LANES) * xb[t][None]
                accs[part, :] = acc.reshape(LANES, LANES)
                if first:
                    for q in range(per):
                        dots_add(vwc, b0c, uc, pc, k * per + q)
                return carry
            return body

        lax.fori_loop(0, half_blocks, block(True), 0)
        sc_b[i, c] = dots_row()
        to_cols(sc_b.at[i, c], sb_sem.at[i])
        lax.fori_loop(half_blocks, blocks, block(False), 0)
        reduce_block(blocks - 1)
        to_cols(sum_b.at[i, c], yb_sem.at[i])

    def matvec_rows(i, j):
        b0r[...] = jnp.where(pos_r > j + 1, c0r[...], 0.0)

        def spread(k):
            return spread_row(b0r[:, pl.ds(pl.multiple_of(k * LANES, LANES), LANES)])

        zero = jnp.zeros((SUB, LANES), F32)

        def products(part, bc, accs_in, base):
            b3 = bc.reshape(GROUPS, SUB, LANES)
            out = []
            for t in range(half_tiles):
                x = tile[part, lanes_of(base + t)].reshape(GROUPS, SUB, LANES)
                out.append(accs_in[t] + jnp.sum(x * b3, axis=0))
            return tuple(out)

        def first(k, state):
            bc, acc = state
            part = pl.ds(pl.multiple_of(k * LANES, LANES), LANES)
            nxt = spread(jnp.minimum(k + 1, blocks - 1))
            xs[part, :] = bc
            dots_add(vwr, b0r, ur, pr, k)
            return nxt, products(part, bc, acc, 0)

        def second(k, acc):
            part = pl.ds(pl.multiple_of(k * LANES, LANES), LANES)
            return products(part, xs[part, :], acc, half_tiles)

        def store(acc, base):
            for t in range(half_tiles):
                sum_a[i, r, base // half_tiles, :, lanes_of(t)] = jnp.sum(acc[t], axis=0, keepdims=True)

        _, acc = lax.fori_loop(0, blocks, first, (spread(0), (zero,) * half_tiles))
        store(acc, 0)
        sc_a[i, r] = dots_row()
        to_rows(sc_a.at[i, r], sa_sem.at[i])
        to_rows(sum_a.at[i, r, 0], ya_sem.at[i, 0])
        acc = lax.fori_loop(0, blocks, second, (zero,) * half_tiles)
        store(acc, half_tiles)
        to_rows(sum_a.at[i, r, 1], ya_sem.at[i, 1])

    def head_advance(j, auh_row):
        advance(j, vwh, c0h, uh, ph, auh, lambda t: auh_row, lambda t: phead[pl.ds(j + 1, 1), :], l128)

    def lane_pick(x, index):
        s = jnp.sum(jnp.where(l128 == index, x, 0.0), axis=1, keepdims=True)
        return jnp.broadcast_to(s, x.shape)

    def picks(j):
        head = vwh[...]
        return (lane_pick(head, j), lane_pick(head, j + 1), lane_pick(c0h[...], j + 1),
                lane_pick(uh[...], j + 1), lane_pick(ph[...], j))

    def scalars(j, sc, picked):
        hj, hj1, c0h1, uj1, pent = picked
        d = jnp.sum(jnp.where(eye40, jnp.broadcast_to(sc, eye40.shape), 0.0), axis=1, keepdims=True)
        d = jnp.broadcast_to(d, eye40.shape)
        vb, wb = d[0:K], d[K:2 * K]
        n0, kp = d[2 * K:2 * K + 1], d[2 * K + 1:2 * K + 2]
        hjv, hjw, hj1v, hj1w = hj[0:K], hj[K:2 * K], hj1[0:K], hj1[K:2 * K]
        last = k16 == j - 1
        tau_prev, bb_prev = srow(0), srow(4)
        kap = 0.5 * tau_prev * kp
        e = 2.0 * kap - pent
        lead = c0h1 + e * uj1
        n1 = jnp.sum(jnp.where(last, vb, 0.0), axis=0, keepdims=True)
        b2 = jnp.maximum(n0 + e * (2.0 * n1 + e * (bb_prev - uj1 * uj1)), 0.0)
        sig = jnp.sqrt(b2 + lead * lead)
        inv = 1.0 / (lead + sig)
        tau = 1.0 + lead / sig
        lk = jnp.where(last, kap, 0.0)
        hjw = hjw - lk * hjv
        hj1w = hj1w - lk * hj1v
        uu = bb_prev + 1.0
        vup = jnp.where(last, uu, vuwu[0:K, :])
        wup = jnp.where(last, kp - kap * uu, vuwu[K:2 * K, :])
        wb = wb - lk * vb
        vu = (vb + e * (vup - hjv - uj1 * hj1v)) * inv + hj1v
        wu = (wb + e * (wup - hjw - uj1 * hj1w)) * inv + hj1w
        beta = tau * vu - hj1v
        alpha = tau * wu - hj1w - lk * beta
        delta = tau * vu
        gamma = tau * wu - lk * delta
        coefc[0:K, :] = alpha
        coefc[K:2 * K, :] = beta
        coefp[0:K, :] = gamma
        coefp[K:2 * K, :] = delta
        vuwu[0:K, :] = vu
        vuwu[K:2 * K, :] = wu
        scal[0:1, :] = tau
        scal[1:2, :] = kap
        scal[2:3, :] = e
        scal[3:4, :] = inv
        scal[4:5, :] = b2 * inv * inv
        scal[5:6, :] = uj1
        coef[0:1, :] = jnp.where(l128 == j, tau, coef[0:1, :])
        coef[1:2, :] = jnp.where(l128 == j, -sig, coef[1:2, :])

    def finish(j, vw, c0, u, p, au_ref, total, row, row_next, pos):
        def au_new(t):
            e, inv, uj1 = srow(2), srow(3), srow(5)
            nxt = row_next(t)
            aq = au_ref[:, lanes_of(t)] - row(t) - uj1 * nxt
            return (total(t) + e * aq) * inv + nxt
        advance(j, vw, c0, u, p, au_ref, au_new, row_next, pos)

    def slot_sum(read, n):
        acc = read(0)
        for s in range(1, n):
            acc = acc + read(s)
        return acc

    def send_v(k, i):
        vout[k, c] = uc[...]
        to_cols(vout.at[k, c], v_sem.at[i])

    def pack_v(i):
        landed(vout.at[0:2, 0:n_col - 1], v_sem.at[i])

    def place_v(i):
        for q in range(2):
            refl[pl.ds(2 * i + q, 1), :] = jnp.concatenate([vout[2 * i + q, cc] for cc in range(n_col)], axis=1)

    def send_red_b(i, j):
        @pl.when(diag)
        def _():
            piece = pl.ds(pl.multiple_of(own_half * rows, LANES), rows)
            red_b[i, 0] = auc[:, piece]
            red_b[i, 1] = rowc[j, :, piece]
            red_b[i, 2] = rowc[j + 1, :, piece]
            to_cols(red_b.at[i], rb_sem.at[i])

    def step_cols(i):
        j = 2 * i
        send_red_b(i, j)

        @pl.when(c == 0)
        def _():
            hd_b[i] = auc[:, 0:LANES]
            to_cols(hd_b.at[i], hb_sem.at[i])

        @pl.when(r == 0)
        def _():
            rowc[j + 2] = headrows[pl.ds(j + 2, 1), :]
            rowc[j + 3] = headrows[pl.ds(j + 3, 1), :]
            to_rows(rowc.at[pl.ds(j + 2, 2)], row_sem.at[i + 1])

        matvec_cols(i, j)

        @pl.when(jnp.logical_and(i == 0, jnp.logical_or(r != 0, c != 0)))
        def _():
            landed(phead, head_sem)

        pl.when(c != 0)(lambda: landed(hd_b.at[i], hb_sem.at[i]))
        head_advance(j - 1, hd_b[i])
        picked = picks(j)
        pl.when(jnp.logical_not(diag))(lambda: landed(red_b.at[i], rb_sem.at[i]))
        advance(j - 1, vwr, c0r, ur, pr, aur, lambda t: red_b[i, 0, :, lanes_of(t)],
                lambda t: red_b[i, 1, :, lanes_of(t)], pos_r)
        landed(sc_b.at[i, 0:n_col - 1], sb_sem.at[i])
        scalars(j, slot_sum(lambda s: sc_b[i, s], n_col), picked)
        landed(sum_b.at[i, 0:n_col - 1], yb_sem.at[i])
        finish(j, vwr, c0r, ur, pr, aur, lambda t: slot_sum(lambda s: sum_b[i, s, :, lanes_of(t)], n_col),
               lambda t: red_b[i, 1, :, lanes_of(t)], lambda t: red_b[i, 2, :, lanes_of(t)], pos_r)

    def step_rows(i):
        j = 2 * i + 1

        @pl.when(diag)
        def _():
            red_a[i, own_half] = aur[...]
            to_rows(red_a.at[i, own_half], ra_sem.at[i, own_half])

        @pl.when(r == 0)
        def _():
            hd_a[i] = aur[:, 0:LANES]
            to_rows(hd_a.at[i], ha_sem.at[i])

        matvec_rows(i, j)

        pl.when(r != 0)(lambda: landed(hd_a.at[i], ha_sem.at[i]))
        head_advance(j - 1, hd_a[i])
        picked = picks(j)
        for h in range(halves):
            pl.when(r != halves * c + h)(lambda h=h: landed(red_a.at[i, h], ra_sem.at[i, h]))
        advance(j - 1, vwc, c0c, uc, pc, auc,
                lambda t: red_a[i, t // rtiles, :, lanes_of(t % rtiles)],
                lambda t: rowc[j, :, lanes_of(t)], pos_c)
        send_v(j - 1, i)

        @pl.when(i > 0)
        def _():
            pack_v(i - 1)
            place_v(i - 1)

        landed(sc_a.at[i, 0:n_row - 1], sa_sem.at[i])
        scalars(j, slot_sum(lambda s: sc_a[i, s], n_row), picked)
        pl.when(r != 0)(lambda: landed(rowc.at[0:2], row_sem.at[i + 1]))
        for h in range(2):
            landed(sum_a.at[i, 0:n_row - 1, 0], ya_sem.at[i, h])
        finish(j, vwc, c0c, uc, pc, auc,
               lambda t: slot_sum(lambda s: sum_a[i, s, t // half_tiles, :, lanes_of(t % half_tiles)], n_row),
               lambda t: rowc[j, :, lanes_of(t)], lambda t: rowc[j + 1, :, lanes_of(t)], pos_c)
        send_v(j, i)

    def pair(i, carry):
        step_cols(i)
        step_rows(i)
        return carry

    lax.fori_loop(0, PAIRS, pair, 0)

    f = PAIRS

    @pl.when(diag)
    def _():
        piece = pl.ds(pl.multiple_of(own_half * rows, LANES), rows)
        red_b[f, 0] = auc[:, piece]
        to_cols(red_b.at[f, 0:1], rb_sem.at[f])

    kp = jnp.sum(uc[...] * pc[...], axis=1, keepdims=True)
    sc_b[f, c] = jnp.broadcast_to(kp, (1, LANES))
    to_cols(sc_b.at[f, c], sb_sem.at[f])
    pl.when(jnp.logical_not(diag))(lambda: landed(red_b.at[f, 0:1], rb_sem.at[f]))
    advance(K - 1, vwr, c0r, ur, pr, aur, lambda t: red_b[f, 0, :, lanes_of(t)],
            lambda t: red_b[f, 0, :, lanes_of(t)], pos_r)
    landed(sc_b.at[f, 0:n_col - 1], sb_sem.at[f])
    kap = 0.5 * srow(0) * slot_sum(lambda s: sc_b[f, s], n_col)
    vwr[2 * K - 1:2 * K, :] = pr[...] - wide(kap, rtiles) * ur[...]
    vwc[2 * K - 1:2 * K, :] = pc[...] - wide(kap, ctiles) * uc[...]
    pack_v(PAIRS - 1)
    place_v(PAIRS - 1)

    def drain(i, carry):
        landed(sum_a.at[i, 0:n_row - 1], ssem)
        landed(sc_a.at[i, 0:n_row - 1], ssem)
        landed(sum_b.at[i, 0:n_col - 1], ssem)
        landed(sc_b.at[i, 0:n_col - 1], ssem)
        for dc in range(1, n_col):
            landed(vout.at[0:2, 0], ssem)

        @pl.when(diag)
        def _():
            for dr in range(1, n_row):
                landed(red_a.at[i, 0], ssem)
            for dc in range(1, n_col):
                landed(red_b.at[i], ssem)

        @pl.when(c == 0)
        def _():
            for dc in range(1, n_col):
                landed(hd_b.at[i], ssem)

        @pl.when(r == 0)
        def _():
            for dr in range(1, n_row):
                landed(hd_a.at[i], ssem)
                landed(rowc.at[0:2], ssem)
        return carry

    lax.fori_loop(0, PAIRS, drain, 0)
    landed(sc_b.at[f, 0:n_col - 1], ssem)

    @pl.when(diag)
    def _():
        for dc in range(1, n_col):
            landed(red_b.at[f, 0:1], ssem)

    @pl.when(r == 0)
    def _():
        for dr in range(1, n_row):
            landed(rowc.at[0:2], ssem)

        @pl.when(c == 0)
        def _():
            for d in range(1, n_row * n_col):
                landed(phead, ssem)


def pieces(x):
    hi = x.astype(jnp.bfloat16)
    rest = x - hi.astype(F32)
    mid = rest.astype(jnp.bfloat16)
    low = (rest - mid.astype(F32)).astype(jnp.bfloat16)
    return hi, mid, low


def update_kernel(rows, cols, tile, vwr, vwc, out, left, right, buf, sem):
    blocks = rows // LANES
    order = ((0, 0), (0, 1), (1, 0), (1, 1), (0, 2), (2, 0))
    two = 2 * K
    lp = pieces(vwr[...])
    wv = jnp.concatenate([vwc[K:two, :], vwc[0:K, :]], axis=0)
    rp = pieces(wv)
    for q, (a, b) in enumerate(order):
        left[q * two:(q + 1) * two, :] = lp[a]
        right[q * two:(q + 1) * two, :] = rp[b]

    def body(i, carry):
        part = pl.ds(pl.multiple_of(i * LANES, LANES), LANES)
        lt = left[:, part]
        change = lax.dot_general(lt, right[...], (((0,), (0,)), ((), ())), preferred_element_type=F32)
        buf[part, :] = tile[part, :] - change
        pltpu.make_async_copy(buf.at[part], out.at[part], sem).start()
        return carry

    lax.fori_loop(0, blocks, body, 0)
    pltpu.make_async_copy(buf, out, sem).wait()


def make_per_device(n_row, n_col):
    def per_device(matrix):
        rows, cols = matrix.shape
        halves = cols // rows
        f32 = F32
        vmem = pl.BlockSpec(memory_space=pltpu.VMEM)
        anyspace = pl.BlockSpec(memory_space=pl.ANY)
        dma = pltpu.SemaphoreType.DMA
        full = n_row * rows

        def kernel(*refs):
            panel_kernel(rows, cols, n_row, n_col, *refs)

        def vm(*shape):
            return pltpu.VMEM(shape, f32)

        tile, refl, vwr, vwc, coef = pl.pallas_call(
            kernel,
            out_shape=(
                jax.ShapeDtypeStruct((rows, cols), f32),
                jax.ShapeDtypeStruct((K, full), f32),
                jax.ShapeDtypeStruct((2 * K, rows), f32),
                jax.ShapeDtypeStruct((2 * K, cols), f32),
                jax.ShapeDtypeStruct((2, LANES), f32),
            ),
            in_specs=[anyspace],
            out_specs=(vmem,) * 5,
            scratch_shapes=[
                vm(HEAD, cols), vm(HEAD, LANES), vm(K + 2, 1, cols), vm(K, n_col, 1, cols),
                vm(PAIRS, n_row, 2, 1, cols // 2), vm(PAIRS, n_col, 1, rows),
                vm(PAIRS, n_row, 1, LANES), vm(PAIRS + 1, n_col, 1, LANES),
                vm(PAIRS, halves, 1, rows), vm(PAIRS + 1, 3, 1, rows),
                vm(PAIRS, 1, LANES), vm(PAIRS, 1, LANES),
                vm(1, rows), vm(1, rows), vm(1, rows), vm(1, rows),
                vm(1, cols), vm(1, cols), vm(1, cols), vm(1, cols),
                vm(1, LANES), vm(1, LANES), vm(1, LANES), vm(1, LANES), vm(2 * K, LANES),
                vm(2 * K, LANES), vm(2 * K, LANES), vm(2 * K, LANES), vm(8, LANES),
                vm(1, rows), vm(1, cols), vm(rows, LANES), vm(rows, LANES), vm(2 * K + SUB, LANES),
                dma((rows // LANES,)), dma, dma, dma((PAIRS + 1,)), dma((PAIRS,)),
                dma((PAIRS, 2)), dma((PAIRS,)), dma((PAIRS, halves)), dma((PAIRS,)),
                dma((PAIRS,)), dma((PAIRS + 1,)), dma((PAIRS + 1,)), dma((PAIRS,)),
                dma,
            ],
            compiler_params=pltpu.CompilerParams(
                collective_id=0, has_side_effects=True, vmem_limit_bytes=24 * 1024 * 1024),
        )(matrix)

        def update(*refs):
            update_kernel(rows, cols, *refs)

        updated = pl.pallas_call(
            update,
            out_shape=jax.ShapeDtypeStruct((rows, cols), f32),
            in_specs=[vmem] * 3,
            out_specs=anyspace,
            scratch_shapes=[
                pltpu.VMEM((12 * K, rows), jnp.bfloat16),
                pltpu.VMEM((12 * K, cols), jnp.bfloat16),
                vm(rows, cols),
                dma,
            ],
            compiler_params=pltpu.CompilerParams(vmem_limit_bytes=24 * 1024 * 1024),
        )(tile, vwr, vwc)
        return updated, refl, coef[:, :K]
    return per_device


def solution(mesh):
    return jax.shard_map(
        make_per_device(mesh.shape["row"], mesh.shape["col"]),
        mesh=mesh,
        in_specs=(P("row", "col"),),
        out_specs=(P("row", "col"), P(), P()),
        check_vma=False,
    )
```

time: 161 us -> 120 us (0.75)
  Pallas kernels: 143 us -> 118 us
  matrix products: 12.1 us -> 0 us
  other arithmetic: 2.86 us -> 0 us
    pallas_call x1 -> x2, Pallas kernels: 143 us -> 118 us  [the longest x1 111 us: per_device(): pl.pallas_call(kernel, out_shape=(jax.ShapeDtypeStruct((rows, cols), f32)...]
    dot_general x1 -> x0, matrix products: 12.1 us -> none  [per_device(): lax.dot_general(big_left, big_right, (((0,), (0,)), ((), ())), preferred_...]
    pallas_call x2 -> x0, other arithmetic: 2.45 us -> none  [per_device(): pl.pallas_call(kernel, out_shape=(jax.ShapeDtypeStruct((K, n_row, 1, rows...]
where the time goes in v1:
time: 120 us
  Pallas kernels  118 us (98%)
  local copies, waits for them, and re-layouts  1.44 us (1%)
    pallas_call x1, Pallas kernels, per_device(): pl.pallas_call(kernel, out_shape=(jax.ShapeDtypeStruct((rows, cols), f32)...  111 us
    pallas_call x1, Pallas kernels, per_device(): pl.pallas_call(update, out_shape=jax.ShapeDtypeStruct((rows, cols), f32),...  7.1 us

profile of v1, /device:TPU:0, one launch (start us, length us, event | category | flops | bytes accessed | tf_op | source)
XLA Modules:
  0.0 120.1 jit_solution(8593232187877543408)
XLA Ops:
  0.6 110.9 %shard_map.38 = (f32[1536,3072]{1,0:T(8,128)S(1)}, f32[16,12288]{1,0:T(8,128)S(1)}, f32[32,1536]{1,0:T(8,128)S(1)}, f32[32,3072]{1,0:T(8,128)S(1)}, f32[2,128]{1,0:T(2,128)S(1)}) custom-call(f32[1536,3072]{1,0:T(8,128)} %refs_0_.1), custom_call_target="tpu_custom_call" | custom-call | tf_op jit(solution)/shard_map/pallas_call | solution.py:536
  111.5 7.1 %shard_map.39 = f32[1536,3072]{1,0:T(8,128)} custom-call(f32[1536,3072]{1,0:T(8,128)S(1)} %get-tuple-element.8.refs_0_, f32[32,1536]{1,0:T(8,128)S(1)} %get-tuple-element.9.refs_1_, f32[32,3072]{1,0:T(8,128)S(1)} %get-tuple-element.10.refs_2_), custom_call_target="tpu_custom_call" | custom-call | tf_op jit(solution)/shard_map/pallas_call | solution.py:570
  118.6 0.9 copy.6
  119.5 0.6 copy.7

commit v2 on v1

v2 whole, which is shorter than its diff:
```python
import jax
import jax.numpy as jnp
from jax import lax
from jax.experimental import pallas as pl
from jax.experimental.pallas import tpu as pltpu
from jax.sharding import PartitionSpec as P

K = 16
PAIRS = K // 2
HEAD = 24
LANES = 128
SUB = 8
GROUPS = LANES // SUB
BATCH = 4
STEP = 3
MESH = pl.DeviceIdType.MESH
F32 = jnp.float32


def lanes_of(t):
    return slice(t * LANES, (t + 1) * LANES)


def tile_rows(n):
    return -(-n // SUB) * SUB


def spread_row(row):
    return jnp.broadcast_to(row, (LANES, LANES)).T


def panel_kernel(rows, cols, n_row, n_col, mat, tile, refl, vwr, vwc, coef,
                 headrows, phead, rowc, vout,
                 sum_a, sum_b, sc_a, sc_b, red_a, red_b, hd_a, hd_b,
                 wr, c0r, ur, pr, aur, qr, wc, c0c, uc, pc, auc, qc, wh, c0h, uh, ph, auh,
                 coefc, coefp, vuwu, scal, b0r, b0c, xs, accs, dacc,
                 load_sem, hrow_sem, head_sem, row_sem, v_sem,
                 ya_sem, sa_sem, ra_sem, ha_sem, yb_sem, sb_sem, rb_sem, hb_sem,
                 ssem):
    halves = cols // rows
    r = lax.axis_index("row")
    c = lax.axis_index("col")
    blocks = rows // LANES
    ctiles = cols // LANES
    rt = rows // LANES
    rp = tile_rows(rt)
    half_blocks = blocks // 2
    diag = r // halves == c
    own_half = lax.rem(r, halves)

    def along_row(dr):
        return (lax.rem(r + dr, n_row), c)

    def along_col(dc):
        return (r, lax.rem(c + dc, n_col))

    def remote(src, dst, sem, device):
        return pltpu.make_async_remote_copy(src, dst, ssem, sem, device_id=device, device_id_type=MESH)

    def landed(ref, sem):
        pltpu.make_async_copy(ref, ref, sem).wait()

    def to_rows(ref, sem):
        for dr in range(1, n_row):
            remote(ref, ref, sem, along_row(dr)).start()

    def to_cols(ref, sem):
        for dc in range(1, n_col):
            remote(ref, ref, sem, along_col(dc)).start()

    def block_rows(k):
        return pl.ds(pl.multiple_of(k * LANES, LANES), LANES)

    def chunk(i):
        part = block_rows(i)
        return pltpu.make_async_copy(mat.at[part], tile.at[part], load_sem.at[i])

    hrow_copy = pltpu.make_async_copy(mat.at[0:HEAD], headrows, hrow_sem)
    pl.when(r == 0)(lambda: hrow_copy.start())

    def start_chunk(i, carry):
        chunk(i).start()
        return carry

    lax.fori_loop(0, blocks, start_chunk, 0)

    barrier = pltpu.get_barrier_semaphore()
    for dr in range(1, n_row):
        pl.semaphore_signal(barrier, inc=1, device_id=along_row(dr), device_id_type=MESH)
    for dc in range(1, n_col):
        pl.semaphore_signal(barrier, inc=1, device_id=along_col(dc), device_id_type=MESH)

    for ref in (wr, c0r, ur, pr, aur, wc, uc, pc, auc, wh, c0h, uh, ph, auh, coefc, coefp, vuwu, scal, coef, vwr, vwc):
        ref[...] = jnp.zeros_like(ref)
    if rp > rt:
        for ref in (rowc, sum_a, sum_b, red_a, red_b):
            lead = ref.shape[:-2]
            ref[tuple(slice(None) for _ in lead) + (slice(rt, rp),)] = jnp.zeros(lead + (rp - rt, LANES), F32)

    def take_row(k):
        x = headrows[pl.ds(k, 1), :]
        for t in range(ctiles):
            rowc[k, t // rt, t % rt:t % rt + 1, :] = x[:, lanes_of(t)]

    @pl.when(r == 0)
    def _():
        hrow_copy.wait()
        take_row(0)
        take_row(1)

    pl.semaphore_wait(barrier, n_row + n_col - 2)

    @pl.when(r == 0)
    def _():
        to_rows(rowc.at[0:2, :, 0:rt], row_sem.at[0])

        @pl.when(c == 0)
        def _():
            phead[...] = headrows[:, 0:LANES]
            for dr in range(1, n_row):
                remote(headrows.at[:, 0:LANES], phead, head_sem, along_row(dr)).start()

    @pl.when(r != 0)
    def _():
        landed(rowc.at[0:2, :, 0:rt], row_sem.at[0])

    def positions(n, base):
        shape = (n, rp, LANES)
        t = lax.broadcasted_iota(jnp.int32, shape, 1)
        x = (lax.broadcasted_iota(jnp.int32, shape, 0) * rt + t) * LANES + lax.broadcasted_iota(jnp.int32, shape, 2)
        return jnp.where(t < rt, x + base, -2)

    l128 = lax.broadcasted_iota(jnp.int32, (1, LANES), 1)
    pos_r = positions(1, r * rows)
    pos_c = positions(halves, c * cols)
    pos_h = jnp.where(lax.broadcasted_iota(jnp.int32, (1, SUB, LANES), 1) < 1,
                      lax.broadcasted_iota(jnp.int32, (1, SUB, LANES), 2), -2)
    k16 = lax.broadcasted_iota(jnp.int32, (K, LANES), 0)
    s40 = lax.broadcasted_iota(jnp.int32, (2 * K + SUB, LANES), 0)
    t40 = lax.broadcasted_iota(jnp.int32, (2 * K + SUB, LANES), 1)
    eye40 = s40 == t40
    diag3 = (lax.broadcasted_iota(jnp.int32, (GROUPS, SUB, LANES), 0) * SUB
             + lax.broadcasted_iota(jnp.int32, (GROUPS, SUB, LANES), 1)
             == lax.broadcasted_iota(jnp.int32, (GROUPS, SUB, LANES), 2))

    def srow(k):
        return scal[k:k + 1, :]

    def splat(ref, k, like):
        return jnp.broadcast_to(ref[k:k + 1, :], like.shape[1:])[None]

    def weighted(w, ref, like):
        acc = w[0] * splat(ref, 0, like)
        for k in range(1, 2 * K):
            acc = acc + w[k] * splat(ref, k, like)
        return acc

    def record(j, w, c0, u, p, au_ref, au, c0n, pn, pos):
        kap, e, inv = splat(scal, 1, pos), splat(scal, 2, pos), splat(scal, 3, pos)
        hot = jnp.where(j >= 0, j + 1, -1)
        u_old = u[...]
        un = jnp.where(pos > j + 1, (c0[...] + e * u_old) * inv, 0.0)
        un = jnp.where(pos == hot, 1.0, un)
        fixed = p[...] - kap * u_old
        w[K + j - 1] = fixed
        w[jnp.maximum(j, 0)] = un
        w[K + j] = pn
        c0[...] = c0n
        u[...] = un
        p[...] = pn
        au_ref[...] = au

    def advance(j, w, c0, u, p, au_ref, au, row, pos):
        ta = splat(scal, 0, pos) * au
        c0n = row - ta + weighted(w, coefc, pos)
        pn = ta - weighted(w, coefp, pos)
        record(j, w, c0, u, p, au_ref, au, c0n, pn, pos)

    def finish(j, w, c0, u, p, au_ref, q, total, row, row_next, pos, b0):
        tau, kap, e, inv, uj1 = (splat(scal, k, pos) for k in (0, 1, 2, 3, 5))
        aq = au_ref[...] - row - uj1 * row_next
        au = (total + e * aq) * inv + row_next
        pn = tau * au - weighted(w, coefp, pos)
        c0n = q[...] + (2.0 * kap * uj1) * u[...] - pn
        record(j, w, c0, u, p, au_ref, au, c0n, pn, pos)
        prepare(j + 1, w, u, p, c0n, b0, pos)

    def fold(x):
        y = x.reshape(-1, SUB, LANES)
        acc = y[0]
        for k in range(1, y.shape[0]):
            acc = acc + y[k]
        return acc

    def prepare(j, w, u, p, c0n, b0, pos):
        x = jnp.where(pos > j + 1, c0n, 0.0)
        b0[...] = x
        for k in range(2 * K):
            dacc[k] = fold(w[k] * x)
        dacc[2 * K] = fold(x * x)
        dacc[2 * K + 1] = fold(u[...] * p[...])

    def dots_row():
        acc = jnp.zeros((SUB, LANES), F32)
        for k in range(2 * K + 2):
            s = jnp.sum(dacc[k], axis=1, keepdims=True)
            acc = jnp.where(jnp.broadcast_to(l128, (SUB, LANES)) == k, s, acc)
        return jnp.sum(acc, axis=0, keepdims=True)

    def matvec_cols(i, j):
        xb = [jnp.broadcast_to(b0c[t // rt, t % rt:t % rt + 1, :], (SUB, LANES)) for t in range(ctiles)]

        def reduce_block(k):
            a = accs[block_rows(k), :].reshape(GROUPS, SUB, LANES)
            s = jnp.sum(a, axis=2, keepdims=True)
            row = jnp.sum(jnp.sum(jnp.where(diag3, s, 0.0), axis=0), axis=0, keepdims=True)
            sum_b[i, c, pl.ds(k, 1), :] = row

        def block(first):
            def body(q, carry):
                for s in range(STEP):
                    pl.when(i == 0)(lambda s=s: chunk(q * STEP + s).wait())
                for s in range(STEP):
                    reduce_block(jnp.maximum(q - 1, 0) * STEP + s)
                if first:
                    sc_b[i, c] = dots_row()
                for s in range(STEP):
                    k = q * STEP + s
                    for g in range(0, GROUPS, BATCH):
                        piece = pl.ds(pl.multiple_of(k * LANES + g * SUB, SUB), BATCH * SUB)
                        acc = jnp.zeros((BATCH, SUB, LANES), F32)
                        for t in range(ctiles):
                            acc = acc + tile[piece, lanes_of(t)].reshape(BATCH, SUB, LANES) * xb[t][None]
                        accs[piece, :] = acc.reshape(BATCH * SUB, LANES)
                return carry
            return body

        lax.fori_loop(0, half_blocks // STEP, block(True), 0)
        to_cols(sc_b.at[i, c], sb_sem.at[i])
        lax.fori_loop(half_blocks // STEP, blocks // STEP, block(False), 0)
        for s in range(STEP):
            reduce_block(blocks - STEP + s)
        to_cols(sum_b.at[i, c, 0:rt], yb_sem.at[i])

    def spread(k):
        xs[block_rows(k), :] = spread_row(b0r[0, pl.ds(k, 1), :])

    def spread_first():
        for s in range(STEP):
            spread(s)

    def matvec_rows(i, j):
        zero = jnp.zeros((SUB, LANES), F32)

        def products(k, accs_in, base):
            out = list(accs_in)
            for g in range(GROUPS):
                piece = pl.ds(pl.multiple_of(k * LANES + g * SUB, SUB), SUB)
                b = xs[piece, :]
                for t in range(rt):
                    out[t] = out[t] + tile[piece, lanes_of(base + t)] * b
            return tuple(out)

        def sweep(h):
            def body(q, acc):
                for s in range(STEP):
                    acc = products(q * STEP + s, acc, h * rt)
                if h == 0:
                    for s in range(STEP):
                        spread(jnp.minimum((q + 1) * STEP + s, blocks - 1))
                    sc_a[i, r] = dots_row()
                return acc
            return body

        for h in range(halves):
            acc = lax.fori_loop(0, blocks // STEP, sweep(h), (zero,) * rt)
            for t in range(rt):
                sum_a[i, r, h, t:t + 1, :] = jnp.sum(acc[t], axis=0, keepdims=True)
            if h == 0:
                to_rows(sc_a.at[i, r], sa_sem.at[i])
            to_rows(sum_a.at[i, r, h, 0:rt], ya_sem.at[i, h])

    def head_advance(j, auh_row):
        advance(j, wh, c0h, uh, ph, auh, auh_row, phead[pl.ds(j + 1, 1), :][None] * jnp.ones((1, SUB, 1), F32), pos_h)

    def lane_pick(x, index):
        s = jnp.sum(jnp.where(l128 == index, x, 0.0), axis=1, keepdims=True)
        return jnp.broadcast_to(s, x.shape)

    def picks(j):
        head = wh[:, 0, 0, :]
        return (lane_pick(head, j), lane_pick(head, j + 1), lane_pick(c0h[0, 0:1, :], j + 1),
                lane_pick(uh[0, 0:1, :], j + 1), lane_pick(ph[0, 0:1, :], j))

    def pre_q(w, q, picked, row_next, pos):
        hj1 = picked[1]
        coefc[0:K, :] = hj1[K:2 * K]
        coefc[K:2 * K, :] = hj1[0:K]
        q[...] = row_next - weighted(w, coefc, pos)

    def scalars(j, sc, picked):
        hj, hj1, c0h1, uj1, pent = picked
        d = jnp.sum(jnp.where(eye40, jnp.broadcast_to(sc, eye40.shape), 0.0), axis=1, keepdims=True)
        d = jnp.broadcast_to(d, eye40.shape)
        vb, wb = d[0:K], d[K:2 * K]
        n0, kp = d[2 * K:2 * K + 1], d[2 * K + 1:2 * K + 2]
        hjv, hjw, hj1v, hj1w = hj[0:K], hj[K:2 * K], hj1[0:K], hj1[K:2 * K]
        last = k16 == j - 1
        tau_prev, bb_prev = srow(0), srow(4)
        kap = 0.5 * tau_prev * kp
        e = 2.0 * kap - pent
        lead = c0h1 + e * uj1
        n1 = jnp.sum(jnp.where(last, vb, 0.0), axis=0, keepdims=True)
        b2 = jnp.maximum(n0 + e * (2.0 * n1 + e * (bb_prev - uj1 * uj1)), 0.0)
        sig = jnp.sqrt(b2 + lead * lead)
        inv = 1.0 / (lead + sig)
        tau = 1.0 + lead / sig
        lk = jnp.where(last, kap, 0.0)
        hjw = hjw - lk * hjv
        hj1w = hj1w - lk * hj1v
        uu = bb_prev + 1.0
        vup = jnp.where(last, uu, vuwu[0:K, :])
        wup = jnp.where(last, kp - kap * uu, vuwu[K:2 * K, :])
        wb = wb - lk * vb
        vu = (vb + e * (vup - hjv - uj1 * hj1v)) * inv + hj1v
        wu = (wb + e * (wup - hjw - uj1 * hj1w)) * inv + hj1w
        beta = tau * vu - hj1v
        alpha = tau * wu - hj1w - lk * beta
        delta = tau * vu
        gamma = tau * wu - lk * delta
        coefc[0:K, :] = alpha
        coefc[K:2 * K, :] = beta
        coefp[0:K, :] = gamma
        coefp[K:2 * K, :] = delta
        vuwu[0:K, :] = vu
        vuwu[K:2 * K, :] = wu
        scal[0:1, :] = tau
        scal[1:2, :] = kap
        scal[2:3, :] = e
        scal[3:4, :] = inv
        scal[4:5, :] = b2 * inv * inv
        scal[5:6, :] = uj1
        coef[0:1, :] = jnp.where(l128 == j, tau, coef[0:1, :])
        coef[1:2, :] = jnp.where(l128 == j, -sig, coef[1:2, :])

    def slot_sum(read, n):
        acc = read(0)
        for s in range(1, n):
            acc = acc + read(s)
        return acc

    def flat(ref):
        n = ref.shape[0]
        return jnp.concatenate([ref[h, t:t + 1, :] for h in range(n) for t in range(rt)], axis=1)

    def send_v(k, i):
        vout[k, c] = uc[...]
        to_cols(vout.at[k, c, :, 0:rt], v_sem.at[i])

    def place_v(i):
        landed(vout.at[0:2, 0:n_col - 1, :, 0:rt], v_sem.at[i])
        for q in range(2):
            refl[pl.ds(2 * i + q, 1), :] = jnp.concatenate(
                [flat(vout.at[2 * i + q, s]) for s in range(n_col)], axis=1)

    def flat_v(k, w, out):
        out[pl.ds(k, 1), :] = flat(w.at[k])

    def send_au_b(i, count, j):
        @pl.when(diag)
        def _():
            red_b[i, 0] = auc[own_half]
            for q in range(1, count):
                red_b[i, q] = rowc[j + q - 1, own_half]
            to_cols(red_b.at[i, 0:count, 0:rt], rb_sem.at[i])

    def step_cols(i):
        j = 2 * i
        send_au_b(i, 3, j)

        @pl.when(c == 0)
        def _():
            hd_b[i] = auc[0:1, 0:SUB]
            to_cols(hd_b.at[i], hb_sem.at[i])

            @pl.when(i == 0)
            def _():
                pl.when(r != 0)(lambda: landed(phead, head_sem))
                to_cols(phead, head_sem)

        matvec_cols(i, j)

        @pl.when(r == 0)
        def _():
            take_row(j + 2)
            take_row(j + 3)
            to_rows(rowc.at[pl.ds(j + 2, 2), :, 0:rt], row_sem.at[i + 1])

        @pl.when(jnp.logical_and(i == 0, c != 0))
        def _():
            landed(phead, head_sem)

        pl.when(c != 0)(lambda: landed(hd_b.at[i], hb_sem.at[i]))
        head_advance(j - 1, hd_b[i])
        picked = picks(j)
        pl.when(jnp.logical_not(diag))(lambda: landed(red_b.at[i, :, 0:rt], rb_sem.at[i]))
        advance(j - 1, wr, c0r, ur, pr, aur, red_b[i, 0:1], red_b[i, 1:2], pos_r)
        pre_q(wr, qr, picked, red_b[i, 2:3], pos_r)
        landed(sc_b.at[i, 0:n_col - 1], sb_sem.at[i])
        scalars(j, slot_sum(lambda s: sc_b[i, s], n_col), picked)
        landed(sum_b.at[i, 0:n_col - 1, 0:rt], yb_sem.at[i])
        finish(j, wr, c0r, ur, pr, aur, qr, slot_sum(lambda s: sum_b[i, s], n_col)[None],
               red_b[i, 1:2], red_b[i, 2:3], pos_r, b0r)
        spread_first()

    def step_rows(i):
        j = 2 * i + 1

        @pl.when(diag)
        def _():
            red_a[i, own_half] = aur[0]
            to_rows(red_a.at[i, own_half, 0:rt], ra_sem.at[i, own_half])

        @pl.when(r == 0)
        def _():
            hd_a[i] = aur[0:1, 0:SUB]
            to_rows(hd_a.at[i], ha_sem.at[i])

        matvec_rows(i, j)

        pl.when(r != 0)(lambda: landed(hd_a.at[i], ha_sem.at[i]))
        head_advance(j - 1, hd_a[i])
        picked = picks(j)
        for h in range(halves):
            pl.when(r != halves * c + h)(lambda h=h: landed(red_a.at[i, h, 0:rt], ra_sem.at[i, h]))
        pl.when(r != 0)(lambda: landed(rowc.at[0:2, :, 0:rt], row_sem.at[i + 1]))
        advance(j - 1, wc, c0c, uc, pc, auc, red_a[i], rowc[j], pos_c)
        pre_q(wc, qc, picked, rowc[j + 1], pos_c)
        send_v(j - 1, i)
        pl.when(i > 0)(lambda: place_v(i - 1))
        landed(sc_a.at[i, 0:n_row - 1], sa_sem.at[i])
        scalars(j, slot_sum(lambda s: sc_a[i, s], n_row), picked)
        for h in range(halves):
            landed(sum_a.at[i, 0:n_row - 1, 0, 0:rt], ya_sem.at[i, h])
        finish(j, wc, c0c, uc, pc, auc, qc, slot_sum(lambda s: sum_a[i, s], n_row),
               rowc[j], rowc[j + 1], pos_c, b0c)
        send_v(j, i)

    def pair(i, carry):
        step_cols(i)
        step_rows(i)
        return carry

    c0c[...] = rowc[0]
    prepare(0, wc, uc, pc, rowc[0], b0c, pos_c)
    lax.fori_loop(0, PAIRS, pair, 0)

    f = PAIRS
    send_au_b(f, 1, K)
    kp = jnp.sum(dacc[2 * K + 1], axis=1, keepdims=True)
    sc_b[f, c] = jnp.sum(jnp.broadcast_to(kp, (SUB, LANES)), axis=0, keepdims=True)
    to_cols(sc_b.at[f, c], sb_sem.at[f])
    for k in range(2 * K - 1):
        flat_v(k, wc, vwc)
    for k in range(2 * K - 2):
        if k != K - 1:
            flat_v(k, wr, vwr)
    pl.when(jnp.logical_not(diag))(lambda: landed(red_b.at[f, 0:1, 0:rt], rb_sem.at[f]))
    advance(K - 1, wr, c0r, ur, pr, aur, red_b[f, 0:1], red_b[f, 0:1], pos_r)
    flat_v(K - 1, wr, vwr)
    flat_v(2 * K - 2, wr, vwr)
    landed(sc_b.at[f, 0:n_col - 1], sb_sem.at[f])
    kap = 0.5 * srow(0) * slot_sum(lambda s: sc_b[f, s], n_col)
    wr[2 * K - 1] = pr[...] - jnp.broadcast_to(kap, (rp, LANES))[None] * ur[...]
    wc[2 * K - 1] = pc[...] - jnp.broadcast_to(kap, (rp, LANES))[None] * uc[...]
    flat_v(2 * K - 1, wr, vwr)
    flat_v(2 * K - 1, wc, vwc)
    place_v(PAIRS - 1)

    def drain(i, carry):
        landed(sum_a.at[i, 0:n_row - 1, :, 0:rt], ssem)
        landed(sc_a.at[i, 0:n_row - 1], ssem)
        landed(sum_b.at[i, 0:n_col - 1, 0:rt], ssem)
        landed(sc_b.at[i, 0:n_col - 1], ssem)
        landed(vout.at[0:2, 0:n_col - 1, :, 0:rt], ssem)

        @pl.when(diag)
        def _():
            for dr in range(1, n_row):
                landed(red_a.at[i, 0, 0:rt], ssem)
            for dc in range(1, n_col):
                landed(red_b.at[i, :, 0:rt], ssem)

        @pl.when(c == 0)
        def _():
            for dc in range(1, n_col):
                landed(hd_b.at[i], ssem)

        @pl.when(r == 0)
        def _():
            for dr in range(1, n_row):
                landed(hd_a.at[i], ssem)
                landed(rowc.at[0:2, :, 0:rt], ssem)
        return carry

    lax.fori_loop(0, PAIRS, drain, 0)
    landed(sc_b.at[f, 0:n_col - 1], ssem)

    @pl.when(diag)
    def _():
        for dc in range(1, n_col):
            landed(red_b.at[f, 0:1, 0:rt], ssem)

    @pl.when(r == 0)
    def _():
        for dr in range(1, n_row):
            landed(rowc.at[0:2, :, 0:rt], ssem)

    @pl.when(c == 0)
    def _():
        for dc in range(1, n_col):
            landed(phead, ssem)

        @pl.when(r == 0)
        def _():
            for dr in range(1, n_row):
                landed(phead, ssem)


def pieces(x):
    hi = x.astype(jnp.bfloat16)
    rest = x - hi.astype(F32)
    mid = rest.astype(jnp.bfloat16)
    low = (rest - mid.astype(F32)).astype(jnp.bfloat16)
    return hi, mid, low


def update_kernel(rows, cols, tile, vwr, vwc, refl, coef, out, refl_out, coef_out, left, right, buf, sem, rsem):
    blocks = rows // LANES
    order = ((0, 0), (0, 1), (1, 0), (1, 1), (0, 2), (2, 0))
    two = 2 * K
    refl_copy = pltpu.make_async_copy(refl, refl_out, rsem)
    refl_copy.start()
    coef_out[...] = coef[:, 0:K]
    lp = pieces(vwr[...])
    wv = jnp.concatenate([vwc[K:two, :], vwc[0:K, :]], axis=0)
    rp = pieces(wv)
    for q, (a, b) in enumerate(order):
        left[q * two:(q + 1) * two, :] = lp[a]
        right[q * two:(q + 1) * two, :] = rp[b]

    def body(i, carry):
        part = pl.ds(pl.multiple_of(i * LANES, LANES), LANES)
        lt = left[:, part]
        change = lax.dot_general(lt, right[...], (((0,), (0,)), ((), ())), preferred_element_type=F32)
        buf[part, :] = tile[part, :] - change
        pltpu.make_async_copy(buf.at[part], out.at[part], sem).start()
        return carry

    lax.fori_loop(0, blocks, body, 0)
    pltpu.make_async_copy(buf, out, sem).wait()
    refl_copy.wait()


def make_per_device(n_row, n_col):
    def per_device(matrix):
        rows, cols = matrix.shape
        halves = cols // rows
        f32 = F32
        vmem = pl.BlockSpec(memory_space=pltpu.VMEM)
        anyspace = pl.BlockSpec(memory_space=pl.ANY)
        dma = pltpu.SemaphoreType.DMA
        full = n_row * rows
        rp = tile_rows(rows // LANES)

        def kernel(*refs):
            panel_kernel(rows, cols, n_row, n_col, *refs)

        def vm(*shape):
            return pltpu.VMEM(shape, f32)

        tile, refl, vwr, vwc, coef = pl.pallas_call(
            kernel,
            out_shape=(
                jax.ShapeDtypeStruct((rows, cols), f32),
                jax.ShapeDtypeStruct((K, full), f32),
                jax.ShapeDtypeStruct((2 * K, rows), f32),
                jax.ShapeDtypeStruct((2 * K, cols), f32),
                jax.ShapeDtypeStruct((2, LANES), f32),
            ),
            in_specs=[anyspace],
            out_specs=(vmem,) * 5,
            scratch_shapes=[
                vm(HEAD, cols), vm(HEAD, LANES), vm(K + 2, halves, rp, LANES), vm(K, n_col, halves, rp, LANES),
                vm(PAIRS, n_row, halves, rp, LANES), vm(PAIRS, n_col, rp, LANES),
                vm(PAIRS, n_row, 1, LANES), vm(PAIRS + 1, n_col, 1, LANES),
                vm(PAIRS, halves, rp, LANES), vm(PAIRS + 1, 3, rp, LANES),
                vm(PAIRS, 1, SUB, LANES), vm(PAIRS, 1, SUB, LANES),
                vm(2 * K, 1, rp, LANES), *[vm(1, rp, LANES)] * 5,
                vm(2 * K, halves, rp, LANES), *[vm(halves, rp, LANES)] * 5,
                vm(2 * K, 1, SUB, LANES), *[vm(1, SUB, LANES)] * 4,
                vm(2 * K, LANES), vm(2 * K, LANES), vm(2 * K, LANES), vm(8, LANES),
                vm(1, rp, LANES), vm(halves, rp, LANES), vm(rows, LANES), vm(rows, LANES),
                vm(2 * K + 2, SUB, LANES),
                dma((rows // LANES,)), dma, dma, dma((PAIRS + 1,)), dma((PAIRS,)),
                dma((PAIRS, halves)), dma((PAIRS,)), dma((PAIRS, halves)), dma((PAIRS,)),
                dma((PAIRS,)), dma((PAIRS + 1,)), dma((PAIRS + 1,)), dma((PAIRS,)),
                dma,
            ],
            compiler_params=pltpu.CompilerParams(
                collective_id=0, has_side_effects=True, vmem_limit_bytes=24 * 1024 * 1024),
        )(matrix)

        def update(*refs):
            update_kernel(rows, cols, *refs)

        return pl.pallas_call(
            update,
            out_shape=(
                jax.ShapeDtypeStruct((rows, cols), f32),
                jax.ShapeDtypeStruct((K, full), f32),
                jax.ShapeDtypeStruct((2, K), f32),
            ),
            in_specs=[vmem] * 5,
            out_specs=(anyspace, anyspace, vmem),
            scratch_shapes=[
                pltpu.VMEM((12 * K, rows), jnp.bfloat16),
                pltpu.VMEM((12 * K, cols), jnp.bfloat16),
                vm(rows, cols),
                dma, dma,
            ],
            compiler_params=pltpu.CompilerParams(vmem_limit_bytes=24 * 1024 * 1024),
        )(tile, vwr, vwc, refl, coef)
    return per_device


def solution(mesh):
    return jax.shard_map(
        make_per_device(mesh.shape["row"], mesh.shape["col"]),
        mesh=mesh,
        in_specs=(P("row", "col"),),
        out_specs=(P("row", "col"), P(), P()),
        check_vma=False,
    )
```

time: 120 us -> 108 us (0.900)
  Pallas kernels: 118 us -> 107 us
  local copies, waits for them, and re-layouts: 1.44 us -> 0 us
    pallas_call x1, Pallas kernels: 111 us -> 99.7 us  [per_device(): pl.pallas_call(kernel, out_shape=(jax.ShapeDtypeStruct((rows, cols), f32)...]
    unnamed x2 -> x0, local copies, waits for them, and re-layouts: 1.44 us -> none
where the time goes in v2:
time: 108 us
  Pallas kernels  107 us (99%)
    pallas_call x1, Pallas kernels, per_device(): pl.pallas_call(kernel, out_shape=(jax.ShapeDtypeStruct((rows, cols), f32)...  99.7 us
    pallas_call x1, Pallas kernels, per_device(): pl.pallas_call(update, out_shape=(jax.ShapeDtypeStruct((rows, cols), f32)...  7.67 us

profile of v2, /device:TPU:0, one launch (start us, length us, event | category | flops | bytes accessed | tf_op | source)
XLA Modules:
  0.0 108.1 jit_solution(3515475297558704716)
XLA Ops:
  0.6 99.7 %shard_map.38 = (f32[1536,3072]{1,0:T(8,128)S(1)}, f32[16,12288]{1,0:T(8,128)S(1)}, f32[32,1536]{1,0:T(8,128)S(1)}, f32[32,3072]{1,0:T(8,128)S(1)}, f32[2,128]{1,0:T(2,128)S(1)}) custom-call(f32[1536,3072]{1,0:T(8,128)} %refs_0_.1), custom_call_target="tpu_custom_call" | custom-call | tf_op jit(solution)/shard_map/pallas_call | solution.py:582
  100.4 7.7 %shard_map.39 = (f32[1536,3072]{1,0:T(8,128)}, f32[16,12288]{1,0:T(8,128)}, f32[2,16]{1,0:T(2,128)}) custom-call(f32[1536,3072]{1,0:T(8,128)S(1)} %get-tuple-element.8.refs_0_, f32[32,1536]{1,0:T(8,128)S(1)} %get-tuple-element.9.refs_1_, f32[32,3072]{1,0:T(8,128)S(1)} %get-tuple-element.10.refs_2_, f32[16,12288]{1,0:T(8,128)S(1)} %get-tuple-element.11.refs_3_, ...), custom_call_target="tpu_custom_call" | custom-call | tf_op jit(solution)/shard_map/pallas_call | solution.py:617

commit v3 on v2

v3 whole, which is shorter than its diff:
```python
import jax
import jax.numpy as jnp
from jax import lax
from jax.experimental import pallas as pl
from jax.experimental.pallas import tpu as pltpu
from jax.sharding import PartitionSpec as P

K = 16
PAIRS = K // 2
HEAD = 24
LANES = 128
SUB = 8
GROUPS = LANES // SUB
BATCH = 4
STEP = 3
MESH = pl.DeviceIdType.MESH
F32 = jnp.float32


def lanes_of(t):
    return slice(t * LANES, (t + 1) * LANES)


def tile_rows(n):
    return -(-n // SUB) * SUB


def spread_row(row):
    return jnp.broadcast_to(row, (LANES, LANES)).T


def panel_kernel(rows, cols, n_row, n_col, mat, tile, refl, vwr, vwc, coef,
                 headrows, phead, rowc, vout,
                 sum_a, sum_b, sc_a, sc_b, red_a, red_b, row_b, hd_a, hd_b,
                 wr, c0r, ur, pr, aur, qr, wc, c0c, uc, pc, auc, qc, wh, c0h, uh, ph, auh,
                 coefc, coefp, vuwu, scal, b0r, b0c, xs, accs, acca, dacc,
                 load_sem, hrow_sem, head_sem, row_sem, v_sem,
                 ya_sem, sa_sem, ra_sem, ha_sem, yb_sem, sb_sem, rb_sem, wb_sem, hb_sem,
                 ssem):
    halves = cols // rows
    r = lax.axis_index("row")
    c = lax.axis_index("col")
    blocks = rows // LANES
    ctiles = cols // LANES
    ut = rows // LANES // 2
    up = tile_rows(ut)
    ht = halves * ut
    diag = r // halves == c
    own_half = lax.rem(r, halves)

    def along_row(dr):
        return (lax.rem(r + dr, n_row), c)

    def along_col(dc):
        return (r, lax.rem(c + dc, n_col))

    def remote(src, dst, sem, device):
        return pltpu.make_async_remote_copy(src, dst, ssem, sem, device_id=device, device_id_type=MESH)

    def landed(ref, sem):
        pltpu.make_async_copy(ref, ref, sem).wait()

    def to_rows(ref, sem):
        for dr in range(1, n_row):
            remote(ref, ref, sem, along_row(dr)).start()

    def to_cols(ref, sem):
        for dc in range(1, n_col):
            remote(ref, ref, sem, along_col(dc)).start()

    def block_rows(k):
        return pl.ds(pl.multiple_of(k * LANES, LANES), LANES)

    def chunk(i):
        part = block_rows(i)
        return pltpu.make_async_copy(mat.at[part], tile.at[part], load_sem.at[i])

    hrow_copy = pltpu.make_async_copy(mat.at[0:HEAD], headrows, hrow_sem)
    pl.when(r == 0)(lambda: hrow_copy.start())

    def start_chunk(i, carry):
        chunk(i).start()
        return carry

    lax.fori_loop(0, blocks, start_chunk, 0)

    barrier = pltpu.get_barrier_semaphore()
    for dr in range(1, n_row):
        pl.semaphore_signal(barrier, inc=1, device_id=along_row(dr), device_id_type=MESH)
    for dc in range(1, n_col):
        pl.semaphore_signal(barrier, inc=1, device_id=along_col(dc), device_id_type=MESH)

    for ref in (wr, c0r, ur, pr, aur, wc, uc, pc, auc, wh, c0h, uh, ph, auh, coefc, coefp, vuwu, scal, coef, vwr, vwc):
        ref[...] = jnp.zeros_like(ref)
    if up > ut:
        for ref in (rowc, sum_a, sum_b, red_a, red_b, row_b):
            lead = ref.shape[:-2]
            ref[tuple(slice(None) for _ in lead) + (slice(ut, up),)] = jnp.zeros(lead + (up - ut, LANES), F32)

    def take_row(k):
        x = headrows[pl.ds(k, 1), :]
        for t in range(ctiles):
            rowc[k, t // ut, t % ut:t % ut + 1, :] = x[:, lanes_of(t)]

    @pl.when(r == 0)
    def _():
        hrow_copy.wait()
        take_row(0)
        take_row(1)

    pl.semaphore_wait(barrier, n_row + n_col - 2)

    @pl.when(r == 0)
    def _():
        to_rows(rowc.at[0:2, :, 0:ut], row_sem.at[0])

        @pl.when(c == 0)
        def _():
            phead[...] = headrows[:, 0:LANES]
            for dr in range(1, n_row):
                remote(headrows.at[:, 0:LANES], phead, head_sem, along_row(dr)).start()

    @pl.when(r != 0)
    def _():
        landed(rowc.at[0:2, :, 0:ut], row_sem.at[0])

    def positions(n, base):
        shape = (n, up, LANES)
        t = lax.broadcasted_iota(jnp.int32, shape, 1)
        x = (lax.broadcasted_iota(jnp.int32, shape, 0) * ut + t) * LANES + lax.broadcasted_iota(jnp.int32, shape, 2)
        return jnp.where(t < ut, x + base, -2)

    l128 = lax.broadcasted_iota(jnp.int32, (1, LANES), 1)
    pos_r = positions(2, r * rows)
    pos_c = positions(2 * halves, c * cols)
    pos_h = jnp.where(lax.broadcasted_iota(jnp.int32, (1, SUB, LANES), 1) < 1,
                      lax.broadcasted_iota(jnp.int32, (1, SUB, LANES), 2), -2)
    k16 = lax.broadcasted_iota(jnp.int32, (K, LANES), 0)
    s40 = lax.broadcasted_iota(jnp.int32, (2 * K + SUB, LANES), 0)
    t40 = lax.broadcasted_iota(jnp.int32, (2 * K + SUB, LANES), 1)
    eye40 = s40 == t40
    diag3 = (lax.broadcasted_iota(jnp.int32, (GROUPS, SUB, LANES), 0) * SUB
             + lax.broadcasted_iota(jnp.int32, (GROUPS, SUB, LANES), 1)
             == lax.broadcasted_iota(jnp.int32, (GROUPS, SUB, LANES), 2))

    def srow(k):
        return scal[k:k + 1, :]

    def splat(ref, k, like):
        return jnp.broadcast_to(ref[k:k + 1, :], like.shape[1:])[None]

    def weighted(w, ref, like, sl=slice(None)):
        acc = w[0, sl] * splat(ref, 0, like)
        for k in range(1, 2 * K):
            acc = acc + w[k, sl] * splat(ref, k, like)
        return acc

    def record(j, w, c0, u, p, au_ref, au, c0n, pn, pos, sl=slice(None)):
        kap, e, inv = splat(scal, 1, pos), splat(scal, 2, pos), splat(scal, 3, pos)
        hot = jnp.where(j >= 0, j + 1, -1)
        u_old = u[sl]
        un = jnp.where(pos > j + 1, (c0[sl] + e * u_old) * inv, 0.0)
        un = jnp.where(pos == hot, 1.0, un)
        fixed = p[sl] - kap * u_old
        w[K + j - 1, sl] = fixed
        w[jnp.maximum(j, 0), sl] = un
        w[K + j, sl] = pn
        c0[sl] = c0n
        u[sl] = un
        p[sl] = pn
        au_ref[sl] = au

    def advance(j, w, c0, u, p, au_ref, au, row, pos):
        ta = splat(scal, 0, pos) * au
        c0n = row - ta + weighted(w, coefc, pos)
        pn = ta - weighted(w, coefp, pos)
        record(j, w, c0, u, p, au_ref, au, c0n, pn, pos)

    def finish(j, h, w, c0, u, p, au_ref, q, total, row, row_next, pos, b0):
        n = pos.shape[0] // 2
        sl = slice(h * n, (h + 1) * n)
        ps = pos[sl]
        tau, kap, e, inv, uj1 = (splat(scal, k, pos) for k in (0, 1, 2, 3, 5))
        nxt = row_next[sl]
        aq = au_ref[sl] - row[sl] - uj1 * nxt
        au = (total + e * aq) * inv + nxt
        pn = tau * au - weighted(w, coefp, pos, sl)
        c0n = q[sl] + (2.0 * kap * uj1) * u[sl] - pn
        record(j, w, c0, u, p, au_ref, au, c0n, pn, ps, sl)
        b0[sl] = jnp.where(ps > j + 2, c0n, 0.0)

    def fold(x):
        y = x.reshape(-1, SUB, LANES)
        acc = y[0]
        for k in range(1, y.shape[0]):
            acc = acc + y[k]
        return acc

    def prepare(w, u, p, b0):
        x = b0[...]
        for k in range(2 * K):
            dacc[k] = fold(w[k] * x)
        dacc[2 * K] = fold(x * x)
        dacc[2 * K + 1] = fold(u[...] * p[...])

    def dots_row():
        acc = jnp.zeros((SUB, LANES), F32)
        for k in range(2 * K + 2):
            s = jnp.sum(dacc[k], axis=1, keepdims=True)
            acc = jnp.where(jnp.broadcast_to(l128, (SUB, LANES)) == k, s, acc)
        return jnp.sum(acc, axis=0, keepdims=True)

    def matvec_cols(i, mid):
        def reduce_block(k, base):
            a = accs[block_rows(k), :].reshape(GROUPS, SUB, LANES)
            s = jnp.sum(a, axis=2, keepdims=True)
            row = jnp.sum(jnp.sum(jnp.where(diag3, s, 0.0), axis=0), axis=0, keepdims=True)
            sum_b[i, c, base, pl.ds(k - base * ut, 1), :] = row

        def products(k, h, xb):
            for g in range(0, GROUPS, BATCH):
                piece = pl.ds(pl.multiple_of(k * LANES + g * SUB, SUB), BATCH * SUB)
                shape = (BATCH, SUB, LANES)
                acc = jnp.zeros(shape, F32) if h == 0 else accs[piece, :].reshape(shape)
                for t in range(ht):
                    acc = acc + tile[piece, lanes_of(h * ht + t)].reshape(shape) * xb[t][None]
                accs[piece, :] = acc.reshape(BATCH * SUB, LANES)

        def wide_x(h):
            ts = [h * ht + t for t in range(ht)]
            return [jnp.broadcast_to(b0c[t // ut, t % ut:t % ut + 1, :], (SUB, LANES)) for t in ts]

        xa = wide_x(0)

        def pass0(q, carry):
            for s in range(STEP):
                pl.when(i == 0)(lambda s=s: chunk(q * STEP + s).wait())
            for s in range(STEP):
                products(q * STEP + s, 0, xa)
            return carry

        lax.fori_loop(0, blocks // STEP, pass0, 0)
        mid()
        xb = wide_x(1)
        turns = ut // STEP
        for a in range(2):
            def pass1(q, carry, a=a, dots=False):
                if dots:
                    sc_b[i, c] = dots_row()
                for s in range(STEP):
                    products(q * STEP + s, 1, xb)
                    if s > 0:
                        reduce_block(q * STEP + s - 1, a)
                return carry

            for q in range(turns):
                early = a == 0 and q == 0
                pass1(a * turns + q, 0, a, early)
                if early:
                    to_cols(sc_b.at[i, c], sb_sem.at[i])
                reduce_block((a * turns + q) * STEP + STEP - 1, a)
            to_cols(sum_b.at[i, c, a, 0:ut], yb_sem.at[i, a])

    def spread(k, a):
        xs[block_rows(k), :] = spread_row(b0r[a, pl.ds(k - a * ut, 1), :])

    def spread_first(a):
        for s in range(STEP):
            spread(a * ut + s, a)

    def matvec_rows(i, mid):
        zero = jnp.zeros((SUB, LANES), F32)

        def products(k, acc, base):
            out = list(acc)
            for g in range(GROUPS):
                piece = pl.ds(pl.multiple_of(k * LANES + g * SUB, SUB), SUB)
                b = xs[piece, :]
                for t in range(len(out)):
                    out[t] = out[t] + tile[piece, lanes_of(base + t)] * b
            return tuple(out)

        def sweep(a, base, spreads):
            def body(q, acc):
                for s in range(STEP):
                    acc = products(q * STEP + s, acc, base)
                    if spreads and s == 0:
                        for n in range(STEP - 1):
                            spread(jnp.minimum((q + 1) * STEP + n, a * ut + ut - 1), a)
                    if spreads and s == 1:
                        spread(jnp.minimum((q + 1) * STEP + STEP - 1, a * ut + ut - 1), a)
                return acc
            return body

        turns = ut // STEP
        acc = lax.fori_loop(0, turns, sweep(0, 0, True), (zero,) * ctiles)
        for t in range(ctiles):
            acca[t] = acc[t]
        mid()
        for h in range(2):
            acc = tuple(acca[h * ht + t] for t in range(ht))
            acc = lax.fori_loop(turns, 2 * turns, sweep(1, h * ht, h == 0), acc)
            for t in range(ht):
                sum_a[i, r, h, t // ut, t % ut:t % ut + 1, :] = jnp.sum(acc[t], axis=0, keepdims=True)
            to_rows(sum_a.at[i, r, h, :, 0:ut], ya_sem.at[i, h])

    def head_advance(j, auh_row):
        advance(j, wh, c0h, uh, ph, auh, auh_row, phead[pl.ds(j + 1, 1), :][None] * jnp.ones((1, SUB, 1), F32), pos_h)

    def lane_pick(x, index):
        s = jnp.sum(jnp.where(l128 == index, x, 0.0), axis=1, keepdims=True)
        return jnp.broadcast_to(s, x.shape)

    def picks(j):
        head = wh[:, 0, 0, :]
        return (lane_pick(head, j), lane_pick(head, j + 1), lane_pick(c0h[0, 0:1, :], j + 1),
                lane_pick(uh[0, 0:1, :], j + 1), lane_pick(ph[0, 0:1, :], j))

    def pre_q(w, q, picked, row_next, pos):
        hj1 = picked[1]
        coefc[0:K, :] = hj1[K:2 * K]
        coefc[K:2 * K, :] = hj1[0:K]
        q[...] = row_next - weighted(w, coefc, pos)

    def scalars(j, sc, picked):
        hj, hj1, c0h1, uj1, pent = picked
        d = jnp.sum(jnp.where(eye40, jnp.broadcast_to(sc, eye40.shape), 0.0), axis=1, keepdims=True)
        d = jnp.broadcast_to(d, eye40.shape)
        vb, wb = d[0:K], d[K:2 * K]
        n0, kp = d[2 * K:2 * K + 1], d[2 * K + 1:2 * K + 2]
        hjv, hjw, hj1v, hj1w = hj[0:K], hj[K:2 * K], hj1[0:K], hj1[K:2 * K]
        last = k16 == j - 1
        tau_prev, bb_prev = srow(0), srow(4)
        kap = 0.5 * tau_prev * kp
        e = 2.0 * kap - pent
        lead = c0h1 + e * uj1
        n1 = jnp.sum(jnp.where(last, vb, 0.0), axis=0, keepdims=True)
        b2 = jnp.maximum(n0 + e * (2.0 * n1 + e * (bb_prev - uj1 * uj1)), 0.0)
        sig = jnp.sqrt(b2 + lead * lead)
        inv = 1.0 / (lead + sig)
        tau = 1.0 + lead / sig
        lk = jnp.where(last, kap, 0.0)
        hjw = hjw - lk * hjv
        hj1w = hj1w - lk * hj1v
        uu = bb_prev + 1.0
        vup = jnp.where(last, uu, vuwu[0:K, :])
        wup = jnp.where(last, kp - kap * uu, vuwu[K:2 * K, :])
        wb = wb - lk * vb
        vu = (vb + e * (vup - hjv - uj1 * hj1v)) * inv + hj1v
        wu = (wb + e * (wup - hjw - uj1 * hj1w)) * inv + hj1w
        beta = tau * vu - hj1v
        alpha = tau * wu - hj1w - lk * beta
        delta = tau * vu
        gamma = tau * wu - lk * delta
        coefc[0:K, :] = alpha
        coefc[K:2 * K, :] = beta
        coefp[0:K, :] = gamma
        coefp[K:2 * K, :] = delta
        vuwu[0:K, :] = vu
        vuwu[K:2 * K, :] = wu
        scal[0:1, :] = tau
        scal[1:2, :] = kap
        scal[2:3, :] = e
        scal[3:4, :] = inv
        scal[4:5, :] = b2 * inv * inv
        scal[5:6, :] = uj1
        coef[0:1, :] = jnp.where(l128 == j, tau, coef[0:1, :])
        coef[1:2, :] = jnp.where(l128 == j, -sig, coef[1:2, :])

    def slot_sum(read, n):
        acc = read(0)
        for s in range(1, n):
            acc = acc + read(s)
        return acc

    def flat(ref):
        n = ref.shape[0]
        return jnp.concatenate([ref[h, t:t + 1, :] for h in range(n) for t in range(ut)], axis=1)

    def send_v(k):
        vout[k, c] = wc[k]
        to_cols(vout.at[k, c, :, 0:ut], v_sem.at[k])

    def place_v(k):
        landed(vout.at[k, 0:n_col - 1, :, 0:ut], v_sem.at[k])
        refl[pl.ds(k, 1), :] = jnp.concatenate([flat(vout.at[k, s]) for s in range(n_col)], axis=1)

    def flat_v(k, w, out):
        out[pl.ds(k, 1), :] = flat(w.at[k])

    piece_c = pl.ds(own_half * 2, 2)

    def send_au_b(i):
        @pl.when(diag)
        def _():
            red_b[i] = auc[piece_c]
            to_cols(red_b.at[i, :, 0:ut], rb_sem.at[i])

    def send_rows_b(i):
        @pl.when(diag)
        def _():
            for q in range(2):
                row_b[i, q] = rowc[2 * i + q, piece_c]
            to_cols(row_b.at[i, :, :, 0:ut], wb_sem.at[i])

    def finish_cols(i, h):
        landed(sum_b.at[i, 0:n_col - 1, 0, 0:ut], yb_sem.at[i, h])
        finish(2 * i, h, wr, c0r, ur, pr, aur, qr, slot_sum(lambda s: sum_b[i, s, h:h + 1], n_col),
               row_b[i, 0], row_b[i, 1], pos_r, b0r)

    def finish_rows(i, h):
        landed(sum_a.at[i, 0:n_row - 1, 0, :, 0:ut], ya_sem.at[i, h])
        finish(2 * i + 1, h, wc, c0c, uc, pc, auc, qc, slot_sum(lambda s: sum_a[i, s, h], n_row),
               rowc[2 * i + 1], rowc[2 * i + 2], pos_c, b0c)

    def step_cols(i):
        j = 2 * i

        def mid():
            pl.when(i > 0)(lambda: finish_rows(jnp.maximum(i - 1, 0), 1))
            prepare(wc, uc, pc, b0c)
            send_au_b(i)

            @pl.when(c == 0)
            def _():
                hd_b[i] = auc[0:1, 0:SUB]
                to_cols(hd_b.at[i], hb_sem.at[i])

                @pl.when(i == 0)
                def _():
                    pl.when(r != 0)(lambda: landed(phead, head_sem))
                    to_cols(phead, head_sem)

        matvec_cols(i, mid)

        @pl.when(r == 0)
        def _():
            take_row(j + 2)
            take_row(j + 3)
            to_rows(rowc.at[pl.ds(j + 2, 2), :, 0:ut], row_sem.at[i + 1])

        @pl.when(jnp.logical_and(i == 0, c != 0))
        def _():
            landed(phead, head_sem)

        pl.when(jnp.logical_not(diag))(lambda: landed(row_b.at[i, :, :, 0:ut], wb_sem.at[i]))
        pl.when(c != 0)(lambda: landed(hd_b.at[i], hb_sem.at[i]))
        head_advance(j - 1, hd_b[i])
        picked = picks(j)
        pl.when(jnp.logical_not(diag))(lambda: landed(red_b.at[i, :, 0:ut], rb_sem.at[i]))
        advance(j - 1, wr, c0r, ur, pr, aur, red_b[i], row_b[i, 0], pos_r)
        pre_q(wr, qr, picked, row_b[i, 1], pos_r)
        landed(sc_b.at[i, 0:n_col - 1], sb_sem.at[i])
        scalars(j, slot_sum(lambda s: sc_b[i, s], n_col), picked)
        finish_cols(i, 0)
        spread_first(0)

    def step_rows(i):
        j = 2 * i + 1

        def mid():
            finish_cols(i, 1)
            spread_first(1)
            prepare(wr, ur, pr, b0r)
            sc_a[i, r] = dots_row()
            to_rows(sc_a.at[i, r], sa_sem.at[i])

            @pl.when(diag)
            def _():
                red_a[i, own_half] = aur[...]
                to_rows(red_a.at[i, own_half, :, 0:ut], ra_sem.at[i, own_half])

            @pl.when(r == 0)
            def _():
                hd_a[i] = aur[0:1, 0:SUB]
                to_rows(hd_a.at[i], ha_sem.at[i])

        matvec_rows(i, mid)

        pl.when(i > 0)(lambda: place_v(jnp.maximum(2 * i - 2, 0)))
        pl.when(i > 1)(lambda: place_v(jnp.maximum(2 * i - 3, 0)))
        pl.when(i > 0)(lambda: send_v(jnp.maximum(2 * i - 1, 0)))
        pl.when(r != 0)(lambda: landed(rowc.at[0:2, :, 0:ut], row_sem.at[i + 1]))
        send_rows_b(i + 1)
        pl.when(r != 0)(lambda: landed(hd_a.at[i], ha_sem.at[i]))
        head_advance(j - 1, hd_a[i])
        picked = picks(j)
        for h in range(halves):
            pl.when(r != halves * c + h)(lambda h=h: landed(red_a.at[i, h, :, 0:ut], ra_sem.at[i, h]))
        advance(j - 1, wc, c0c, uc, pc, auc, jnp.concatenate([red_a[i, h] for h in range(halves)], axis=0),
                rowc[j], pos_c)
        send_v(j - 1)
        pre_q(wc, qc, picked, rowc[j + 1], pos_c)
        landed(sc_a.at[i, 0:n_row - 1], sa_sem.at[i])
        scalars(j, slot_sum(lambda s: sc_a[i, s], n_row), picked)
        finish_rows(i, 0)

    def pair(i, carry):
        step_cols(i)
        step_rows(i)
        return carry

    c0c[...] = rowc[0]
    b0c[...] = jnp.where(pos_c > 1, rowc[0], 0.0)
    send_rows_b(0)
    lax.fori_loop(0, PAIRS, pair, 0)

    f = PAIRS
    finish_rows(f - 1, 1)
    send_au_b(f)
    kp = jnp.sum(fold(uc[...] * pc[...]), axis=1, keepdims=True)
    sc_b[f, c] = jnp.sum(jnp.broadcast_to(kp, (SUB, LANES)), axis=0, keepdims=True)
    to_cols(sc_b.at[f, c], sb_sem.at[f])
    send_v(K - 1)
    for k in range(2 * K - 1):
        flat_v(k, wc, vwc)
    for k in range(2 * K - 2):
        if k != K - 1:
            flat_v(k, wr, vwr)
    place_v(K - 3)
    place_v(K - 2)
    pl.when(jnp.logical_not(diag))(lambda: landed(row_b.at[f, :, :, 0:ut], wb_sem.at[f]))
    pl.when(jnp.logical_not(diag))(lambda: landed(red_b.at[f, :, 0:ut], rb_sem.at[f]))
    advance(K - 1, wr, c0r, ur, pr, aur, red_b[f], row_b[f, 0], pos_r)
    flat_v(K - 1, wr, vwr)
    flat_v(2 * K - 2, wr, vwr)
    landed(sc_b.at[f, 0:n_col - 1], sb_sem.at[f])
    kap = 0.5 * srow(0) * slot_sum(lambda s: sc_b[f, s], n_col)
    wr[2 * K - 1] = pr[...] - jnp.broadcast_to(kap, (up, LANES))[None] * ur[...]
    wc[2 * K - 1] = pc[...] - jnp.broadcast_to(kap, (up, LANES))[None] * uc[...]
    flat_v(2 * K - 1, wr, vwr)
    flat_v(2 * K - 1, wc, vwc)
    place_v(K - 1)

    def drain(i, carry):
        landed(sum_a.at[i, 0:n_row - 1, :, :, 0:ut], ssem)
        landed(sc_a.at[i, 0:n_row - 1], ssem)
        landed(sum_b.at[i, 0:n_col - 1, :, 0:ut], ssem)
        landed(sc_b.at[i, 0:n_col - 1], ssem)
        landed(vout.at[0:2, 0:n_col - 1, :, 0:ut], ssem)

        @pl.when(diag)
        def _():
            for dr in range(1, n_row):
                landed(red_a.at[i, 0, :, 0:ut], ssem)
            for dc in range(1, n_col):
                landed(red_b.at[i, :, 0:ut], ssem)
                landed(row_b.at[i, :, :, 0:ut], ssem)

        @pl.when(c == 0)
        def _():
            for dc in range(1, n_col):
                landed(hd_b.at[i], ssem)

        @pl.when(r == 0)
        def _():
            for dr in range(1, n_row):
                landed(hd_a.at[i], ssem)
                landed(rowc.at[0:2, :, 0:ut], ssem)
        return carry

    lax.fori_loop(0, PAIRS, drain, 0)
    landed(sc_b.at[f, 0:n_col - 1], ssem)

    @pl.when(diag)
    def _():
        for dc in range(1, n_col):
            landed(red_b.at[f, :, 0:ut], ssem)
            landed(row_b.at[f, :, :, 0:ut], ssem)

    @pl.when(r == 0)
    def _():
        for dr in range(1, n_row):
            landed(rowc.at[0:2, :, 0:ut], ssem)

    @pl.when(c == 0)
    def _():
        for dc in range(1, n_col):
            landed(phead, ssem)

        @pl.when(r == 0)
        def _():
            for dr in range(1, n_row):
                landed(phead, ssem)


def pieces(x):
    hi = x.astype(jnp.bfloat16)
    rest = x - hi.astype(F32)
    mid = rest.astype(jnp.bfloat16)
    low = (rest - mid.astype(F32)).astype(jnp.bfloat16)
    return hi, mid, low


def update_kernel(rows, cols, tile, vwr, vwc, refl, coef, out, refl_out, coef_out, left, right, buf, sem, rsem):
    blocks = rows // LANES
    order = ((0, 0), (0, 1), (1, 0), (1, 1), (0, 2), (2, 0))
    two = 2 * K
    refl_copy = pltpu.make_async_copy(refl, refl_out, rsem)
    refl_copy.start()
    coef_out[...] = coef[:, 0:K]
    lp = pieces(vwr[...])
    wv = jnp.concatenate([vwc[K:two, :], vwc[0:K, :]], axis=0)
    rp = pieces(wv)
    for q, (a, b) in enumerate(order):
        left[q * two:(q + 1) * two, :] = lp[a]
        right[q * two:(q + 1) * two, :] = rp[b]

    def body(i, carry):
        part = pl.ds(pl.multiple_of(i * LANES, LANES), LANES)
        lt = left[:, part]
        change = lax.dot_general(lt, right[...], (((0,), (0,)), ((), ())), preferred_element_type=F32)
        buf[part, :] = tile[part, :] - change
        pltpu.make_async_copy(buf.at[part], out.at[part], sem).start()
        return carry

    lax.fori_loop(0, blocks, body, 0)
    pltpu.make_async_copy(buf, out, sem).wait()
    refl_copy.wait()


def make_per_device(n_row, n_col):
    def per_device(matrix):
        rows, cols = matrix.shape
        halves = cols // rows
        f32 = F32
        vmem = pl.BlockSpec(memory_space=pltpu.VMEM)
        anyspace = pl.BlockSpec(memory_space=pl.ANY)
        dma = pltpu.SemaphoreType.DMA
        full = n_row * rows
        up = tile_rows(rows // LANES // 2)

        def kernel(*refs):
            panel_kernel(rows, cols, n_row, n_col, *refs)

        def vm(*shape):
            return pltpu.VMEM(shape, f32)

        tile, refl, vwr, vwc, coef = pl.pallas_call(
            kernel,
            out_shape=(
                jax.ShapeDtypeStruct((rows, cols), f32),
                jax.ShapeDtypeStruct((K, full), f32),
                jax.ShapeDtypeStruct((2 * K, rows), f32),
                jax.ShapeDtypeStruct((2 * K, cols), f32),
                jax.ShapeDtypeStruct((2, LANES), f32),
            ),
            in_specs=[anyspace],
            out_specs=(vmem,) * 5,
            scratch_shapes=[
                vm(HEAD, cols), vm(HEAD, LANES), vm(K + 2, 2 * halves, up, LANES),
                vm(K, n_col, 2 * halves, up, LANES),
                vm(PAIRS, n_row, 2, halves, up, LANES), vm(PAIRS, n_col, 2, up, LANES),
                vm(PAIRS, n_row, 1, LANES), vm(PAIRS + 1, n_col, 1, LANES),
                vm(PAIRS, halves, 2, up, LANES), vm(PAIRS + 1, 2, up, LANES), vm(PAIRS + 1, 2, 2, up, LANES),
                vm(PAIRS, 1, SUB, LANES), vm(PAIRS, 1, SUB, LANES),
                vm(2 * K, 2, up, LANES), *[vm(2, up, LANES)] * 5,
                vm(2 * K, 2 * halves, up, LANES), *[vm(2 * halves, up, LANES)] * 5,
                vm(2 * K, 1, SUB, LANES), *[vm(1, SUB, LANES)] * 4,
                vm(2 * K, LANES), vm(2 * K, LANES), vm(2 * K, LANES), vm(8, LANES),
                vm(2, up, LANES), vm(2 * halves, up, LANES), vm(rows, LANES), vm(rows, LANES),
                vm(cols // LANES, SUB, LANES), vm(2 * K + 2, SUB, LANES),
                dma((rows // LANES,)), dma, dma, dma((PAIRS + 1,)), dma((K,)),
                dma((PAIRS, 2)), dma((PAIRS,)), dma((PAIRS, halves)), dma((PAIRS,)),
                dma((PAIRS, 2)), dma((PAIRS + 1,)), dma((PAIRS + 1,)), dma((PAIRS + 1,)), dma((PAIRS,)),
                dma,
            ],
            compiler_params=pltpu.CompilerParams(
                collective_id=0, has_side_effects=True, vmem_limit_bytes=24 * 1024 * 1024),
        )(matrix)

        def update(*refs):
            update_kernel(rows, cols, *refs)

        return pl.pallas_call(
            update,
            out_shape=(
                jax.ShapeDtypeStruct((rows, cols), f32),
                jax.ShapeDtypeStruct((K, full), f32),
                jax.ShapeDtypeStruct((2, K), f32),
            ),
            in_specs=[vmem] * 5,
            out_specs=(anyspace, anyspace, vmem),
            scratch_shapes=[
                pltpu.VMEM((12 * K, rows), jnp.bfloat16),
                pltpu.VMEM((12 * K, cols), jnp.bfloat16),
                vm(rows, cols),
                dma, dma,
            ],
            compiler_params=pltpu.CompilerParams(vmem_limit_bytes=24 * 1024 * 1024),
        )(tile, vwr, vwc, refl, coef)
    return per_device


def solution(mesh):
    return jax.shard_map(
        make_per_device(mesh.shape["row"], mesh.shape["col"]),
        mesh=mesh,
        in_specs=(P("row", "col"),),
        out_specs=(P("row", "col"), P(), P()),
        check_vma=False,
    )
```

time: 108 us -> 102 us (0.944)
  Pallas kernels: 107 us -> 101 us
    pallas_call x1, Pallas kernels: 99.7 us -> 93.5 us  [per_device(): pl.pallas_call(kernel, out_shape=(jax.ShapeDtypeStruct((rows, cols), f32)...]
where the time goes in v3:
time: 102 us
  Pallas kernels  101 us (99%)
    pallas_call x1, Pallas kernels, per_device(): pl.pallas_call(kernel, out_shape=(jax.ShapeDtypeStruct((rows, cols), f32)...  93.5 us
    pallas_call x1, Pallas kernels, per_device(): pl.pallas_call(update, out_shape=(jax.ShapeDtypeStruct((rows, cols), f32)...  7.67 us

profile of v3, /device:TPU:0, one launch (start us, length us, event | category | flops | bytes accessed | tf_op | source)
XLA Modules:
  0.0 101.8 jit_solution(6361434209294064110)
XLA Ops:
  0.6 93.5 %shard_map.38 = (f32[1536,3072]{1,0:T(8,128)S(1)}, f32[16,12288]{1,0:T(8,128)S(1)}, f32[32,1536]{1,0:T(8,128)S(1)}, f32[32,3072]{1,0:T(8,128)S(1)}, f32[2,128]{1,0:T(2,128)S(1)}) custom-call(f32[1536,3072]{1,0:T(8,128)} %refs_0_.1), custom_call_target="tpu_custom_call" | custom-call | tf_op jit(solution)/shard_map/pallas_call | solution.py:639
  94.2 7.7 %shard_map.39 = (f32[1536,3072]{1,0:T(8,128)}, f32[16,12288]{1,0:T(8,128)}, f32[2,16]{1,0:T(2,128)}) custom-call(f32[1536,3072]{1,0:T(8,128)S(1)} %get-tuple-element.8.refs_0_, f32[32,1536]{1,0:T(8,128)S(1)} %get-tuple-element.9.refs_1_, f32[32,3072]{1,0:T(8,128)S(1)} %get-tuple-element.10.refs_2_, f32[16,12288]{1,0:T(8,128)S(1)} %get-tuple-element.11.refs_3_, ...), custom_call_target="tpu_custom_call" | custom-call | tf_op jit(solution)/shard_map/pallas_call | solution.py:675

commit v4 on v3

--- a/solution.py
+++ b/solution.py
@@ -60,13 +60,24 @@
     def landed(ref, sem):
         pltpu.make_async_copy(ref, ref, sem).wait()
 
+    def far_first(me, n):
+        low = 2 * me < n
+        out = []
+        for t in range(n - 1):
+            down = n - 1 - t
+            out.append(jnp.where(low, jnp.where(down > me, down, down - 1), jnp.where(t < me, t, t + 1)))
+        return out
+
+    row_targets = far_first(r, n_row)
+    col_targets = far_first(c, n_col)
+
     def to_rows(ref, sem):
-        for dr in range(1, n_row):
-            remote(ref, ref, sem, along_row(dr)).start()
+        for t in row_targets:
+            remote(ref, ref, sem, (t, c)).start()
 
     def to_cols(ref, sem):
-        for dc in range(1, n_col):
-            remote(ref, ref, sem, along_col(dc)).start()
+        for t in col_targets:
+            remote(ref, ref, sem, (r, t)).start()
 
     def block_rows(k):
         return pl.ds(pl.multiple_of(k * LANES, LANES), LANES)
@@ -112,7 +123,9 @@
 
     @pl.when(r == 0)
     def _():
-        to_rows(rowc.at[0:2, :, 0:ut], row_sem.at[0])
+        to_rows(rowc.at[0, 0:halves, 0:ut], row_sem.at[PAIRS + 1])
+        to_rows(rowc.at[0, halves:2 * halves, 0:ut], row_sem.at[PAIRS + 2])
+        to_rows(rowc.at[1, :, 0:ut], row_sem.at[0])
 
         @pl.when(c == 0)
         def _():
@@ -122,7 +135,7 @@
 
     @pl.when(r != 0)
     def _():
-        landed(rowc.at[0:2, :, 0:ut], row_sem.at[0])
+        landed(rowc.at[0, 0:halves, 0:ut], row_sem.at[PAIRS + 1])
 
     def positions(n, base):
         shape = (n, up, LANES)
@@ -280,26 +293,38 @@
                     out[t] = out[t] + tile[piece, lanes_of(base + t)] * b
             return tuple(out)
 
-        def sweep(a, base, spreads):
+        def ahead(k, a):
+            spread(jnp.minimum(k, a * ut + ut - 1), a)
+
+        def sweep(a, base, lead, dots=False):
             def body(q, acc):
+                if dots:
+                    sc_a[i, r] = dots_row()
                 for s in range(STEP):
                     acc = products(q * STEP + s, acc, base)
-                    if spreads and s == 0:
+                    if lead and s == 0:
                         for n in range(STEP - 1):
-                            spread(jnp.minimum((q + 1) * STEP + n, a * ut + ut - 1), a)
-                    if spreads and s == 1:
-                        spread(jnp.minimum((q + 1) * STEP + STEP - 1, a * ut + ut - 1), a)
+                            ahead(q * STEP + lead + n, a)
+                    if lead and s == 1:
+                        ahead(q * STEP + lead + STEP - 1, a)
                 return acc
             return body
 
         turns = ut // STEP
-        acc = lax.fori_loop(0, turns, sweep(0, 0, True), (zero,) * ctiles)
+        acc = lax.fori_loop(0, turns, sweep(0, 0, 1), (zero,) * ctiles)
         for t in range(ctiles):
             acca[t] = acc[t]
         mid()
         for h in range(2):
             acc = tuple(acca[h * ht + t] for t in range(ht))
-            acc = lax.fori_loop(turns, 2 * turns, sweep(1, h * ht, h == 0), acc)
+            lead = STEP if h == 0 else 0
+            if h == 0:
+                cut = turns + jnp.minimum(i + 1, 1)
+                acc = lax.fori_loop(turns, cut, sweep(1, 0, lead, True), acc)
+                to_rows(sc_a.at[i, r], sa_sem.at[i])
+                acc = lax.fori_loop(cut, 2 * turns, sweep(1, 0, lead), acc)
+            else:
+                acc = lax.fori_loop(turns, 2 * turns, sweep(1, h * ht, 0), acc)
             for t in range(ht):
                 sum_a[i, r, h, t // ut, t % ut:t % ut + 1, :] = jnp.sum(acc[t], axis=0, keepdims=True)
             to_rows(sum_a.at[i, r, h, :, 0:ut], ya_sem.at[i, h])
@@ -413,10 +438,26 @@
         finish(2 * i + 1, h, wc, c0c, uc, pc, auc, qc, slot_sum(lambda s: sum_a[i, s, h], n_row),
                rowc[2 * i + 1], rowc[2 * i + 2], pos_c, b0c)
 
+    def start_half(h):
+        sl = slice(h * halves, (h + 1) * halves)
+        x = rowc[0, sl]
+        c0c[sl] = x
+        b0c[sl] = jnp.where(pos_c[sl] > 1, x, 0.0)
+
     def step_cols(i):
         j = 2 * i
 
         def mid():
+            @pl.when(i == 0)
+            def _():
+                @pl.when(r != 0)
+                def _():
+                    landed(rowc.at[0, 0:halves, 0:ut], row_sem.at[PAIRS + 2])
+                    landed(rowc.at[1, :, 0:ut], row_sem.at[0])
+
+                start_half(1)
+                send_rows_b(0)
+
             pl.when(i > 0)(lambda: finish_rows(jnp.maximum(i - 1, 0), 1))
             prepare(wc, uc, pc, b0c)
             send_au_b(i)
@@ -453,7 +494,7 @@
         landed(sc_b.at[i, 0:n_col - 1], sb_sem.at[i])
         scalars(j, slot_sum(lambda s: sc_b[i, s], n_col), picked)
         finish_cols(i, 0)
-        spread_first(0)
+        spread(0, 0)
 
     def step_rows(i):
         j = 2 * i + 1
@@ -462,8 +503,6 @@
             finish_cols(i, 1)
             spread_first(1)
             prepare(wr, ur, pr, b0r)
-            sc_a[i, r] = dots_row()
-            to_rows(sc_a.at[i, r], sa_sem.at[i])
 
             @pl.when(diag)
             def _():
@@ -500,9 +539,7 @@
         step_rows(i)
         return carry
 
-    c0c[...] = rowc[0]
-    b0c[...] = jnp.where(pos_c > 1, rowc[0], 0.0)
-    send_rows_b(0)
+    start_half(0)
     lax.fori_loop(0, PAIRS, pair, 0)
 
     f = PAIRS
@@ -660,7 +697,7 @@
                 vm(2 * K, LANES), vm(2 * K, LANES), vm(2 * K, LANES), vm(8, LANES),
                 vm(2, up, LANES), vm(2 * halves, up, LANES), vm(rows, LANES), vm(rows, LANES),
                 vm(cols // LANES, SUB, LANES), vm(2 * K + 2, SUB, LANES),
-                dma((rows // LANES,)), dma, dma, dma((PAIRS + 1,)), dma((K,)),
+                dma((rows // LANES,)), dma, dma, dma((PAIRS + 3,)), dma((K,)),
                 dma((PAIRS, 2)), dma((PAIRS,)), dma((PAIRS, halves)), dma((PAIRS,)),
                 dma((PAIRS, 2)), dma((PAIRS + 1,)), dma((PAIRS + 1,)), dma((PAIRS + 1,)), dma((PAIRS,)),
                 dma,

time: 102 us -> 100 us (0.980)
  Pallas kernels: 101 us -> 99.3 us
    pallas_call x1, Pallas kernels: 93.5 us -> 91.6 us  [per_device(): pl.pallas_call(kernel, out_shape=(jax.ShapeDtypeStruct((rows, cols), f32)...]
where the time goes in v4:
time: 100 us; the launch traced here: 99.9 us
  Pallas kernels  99.3 us (99%)
    pallas_call x1, Pallas kernels, per_device(): pl.pallas_call(kernel, out_shape=(jax.ShapeDtypeStruct((rows, cols), f32)...  91.6 us
    pallas_call x1, Pallas kernels, per_device(): pl.pallas_call(update, out_shape=(jax.ShapeDtypeStruct((rows, cols), f32)...  7.67 us

profile of v4, /device:TPU:0, one launch (start us, length us, event | category | flops | bytes accessed | tf_op | source)
XLA Modules:
  0.0 99.9 jit_solution(3204764591605764531)
XLA Ops:
  0.6 91.6 %shard_map.38 = (f32[1536,3072]{1,0:T(8,128)S(1)}, f32[16,12288]{1,0:T(8,128)S(1)}, f32[32,1536]{1,0:T(8,128)S(1)}, f32[32,3072]{1,0:T(8,128)S(1)}, f32[2,128]{1,0:T(2,128)S(1)}) custom-call(f32[1536,3072]{1,0:T(8,128)} %refs_0_.1), custom_call_target="tpu_custom_call" | custom-call | tf_op jit(solution)/shard_map/pallas_call | solution.py:676
  92.2 7.7 %shard_map.39 = (f32[1536,3072]{1,0:T(8,128)}, f32[16,12288]{1,0:T(8,128)}, f32[2,16]{1,0:T(2,128)}) custom-call(f32[1536,3072]{1,0:T(8,128)S(1)} %get-tuple-element.8.refs_0_, f32[32,1536]{1,0:T(8,128)S(1)} %get-tuple-element.9.refs_1_, f32[32,3072]{1,0:T(8,128)S(1)} %get-tuple-element.10.refs_2_, f32[16,12288]{1,0:T(8,128)S(1)} %get-tuple-element.11.refs_3_, ...), custom_call_target="tpu_custom_call" | custom-call | tf_op jit(solution)/shard_map/pallas_call | solution.py:712

commit v5 on v4

--- a/solution.py
+++ b/solution.py
@@ -11,7 +11,7 @@
 LANES = 128
 SUB = 8
 GROUPS = LANES // SUB
-BATCH = 4
+BATCH = 8
 STEP = 3
 MESH = pl.DeviceIdType.MESH
 F32 = jnp.float32
@@ -556,6 +556,34 @@
             flat_v(k, wr, vwr)
     place_v(K - 3)
     place_v(K - 2)
+    def drain(i, carry):
+        landed(sum_a.at[i, 0:n_row - 1, :, :, 0:ut], ssem)
+        landed(sc_a.at[i, 0:n_row - 1], ssem)
+        landed(sum_b.at[i, 0:n_col - 1, :, 0:ut], ssem)
+        landed(sc_b.at[i, 0:n_col - 1], ssem)
+        landed(vout.at[0:2, 0:n_col - 1, :, 0:ut], ssem)
+
+        @pl.when(diag)
+        def _():
+            for dr in range(1, n_row):
+                landed(red_a.at[i, 0, :, 0:ut], ssem)
+            for dc in range(1, n_col):
+                landed(red_b.at[i, :, 0:ut], ssem)
+                landed(row_b.at[i, :, :, 0:ut], ssem)
+
+        @pl.when(c == 0)
+        def _():
+            for dc in range(1, n_col):
+                landed(hd_b.at[i], ssem)
+
+        @pl.when(r == 0)
+        def _():
+            for dr in range(1, n_row):
+                landed(hd_a.at[i], ssem)
+                landed(rowc.at[0:2, :, 0:ut], ssem)
+        return carry
+
+    lax.fori_loop(0, PAIRS, drain, 0)
     pl.when(jnp.logical_not(diag))(lambda: landed(row_b.at[f, :, :, 0:ut], wb_sem.at[f]))
     pl.when(jnp.logical_not(diag))(lambda: landed(red_b.at[f, :, 0:ut], rb_sem.at[f]))
     advance(K - 1, wr, c0r, ur, pr, aur, red_b[f], row_b[f, 0], pos_r)
@@ -569,34 +597,6 @@
     flat_v(2 * K - 1, wc, vwc)
     place_v(K - 1)
 
-    def drain(i, carry):
-        landed(sum_a.at[i, 0:n_row - 1, :, :, 0:ut], ssem)
-        landed(sc_a.at[i, 0:n_row - 1], ssem)
-        landed(sum_b.at[i, 0:n_col - 1, :, 0:ut], ssem)
-        landed(sc_b.at[i, 0:n_col - 1], ssem)
-        landed(vout.at[0:2, 0:n_col - 1, :, 0:ut], ssem)
-
-        @pl.when(diag)
-        def _():
-            for dr in range(1, n_row):
-                landed(red_a.at[i, 0, :, 0:ut], ssem)
-            for dc in range(1, n_col):
-                landed(red_b.at[i, :, 0:ut], ssem)
-                landed(row_b.at[i, :, :, 0:ut], ssem)
-
-        @pl.when(c == 0)
-        def _():
-            for dc in range(1, n_col):
-                landed(hd_b.at[i], ssem)
-
-        @pl.when(r == 0)
-        def _():
-            for dr in range(1, n_row):
-                landed(hd_a.at[i], ssem)
-                landed(rowc.at[0:2, :, 0:ut], ssem)
-        return carry
-
-    lax.fori_loop(0, PAIRS, drain, 0)
     landed(sc_b.at[f, 0:n_col - 1], ssem)
 
     @pl.when(diag)

time: 100 us -> 100 us (level)
  no operation moved by 1% of the time
where the time goes in v5:
time: 100 us; the launch traced here: 99.9 us
  Pallas kernels  99.2 us (99%)
    pallas_call x1, Pallas kernels, per_device(): pl.pallas_call(kernel, out_shape=(jax.ShapeDtypeStruct((rows, cols), f32)...  91.6 us
    pallas_call x1, Pallas kernels, per_device(): pl.pallas_call(update, out_shape=(jax.ShapeDtypeStruct((rows, cols), f32)...  7.67 us

profile of v5, /device:TPU:0, one launch (start us, length us, event | category | flops | bytes accessed | tf_op | source)
XLA Modules:
  0.0 99.9 jit_solution(17187367515887021894)
XLA Ops:
  0.6 91.6 %shard_map.38 = (f32[1536,3072]{1,0:T(8,128)S(1)}, f32[16,12288]{1,0:T(8,128)S(1)}, f32[32,1536]{1,0:T(8,128)S(1)}, f32[32,3072]{1,0:T(8,128)S(1)}, f32[2,128]{1,0:T(2,128)S(1)}) custom-call(f32[1536,3072]{1,0:T(8,128)} %refs_0_.1), custom_call_target="tpu_custom_call" | custom-call | tf_op jit(solution)/shard_map/pallas_call | solution.py:676
  92.2 7.7 %shard_map.39 = (f32[1536,3072]{1,0:T(8,128)}, f32[16,12288]{1,0:T(8,128)}, f32[2,16]{1,0:T(2,128)}) custom-call(f32[1536,3072]{1,0:T(8,128)S(1)} %get-tuple-element.8.refs_0_, f32[32,1536]{1,0:T(8,128)S(1)} %get-tuple-element.9.refs_1_, f32[32,3072]{1,0:T(8,128)S(1)} %get-tuple-element.10.refs_2_, f32[16,12288]{1,0:T(8,128)S(1)} %get-tuple-element.11.refs_3_, ...), custom_call_target="tpu_custom_call" | custom-call | tf_op jit(solution)/shard_map/pallas_call | solution.py:712
